TPU v7x, 32 devices: a whole 2x2x4 slice. The times are simulated.
32 devices in a mesh: batch: 8 (over y, x, core), chan: 4 (over z).
Axes of the slice: x: 2, y: 2, z: 4, core: 2. Of those that a mesh axis runs over, the one named last changes fastest.
Arguments:
- images: bfloat16 [64, 14, 14, 4096], P('batch', None, None, 'chan'), may hold values from -12 to 12, as said below
- reduce_weight: bfloat16 [4096, 1024], P(None, 'chan'), may hold values from -0.09375 to 0.09375
- reduce_gain: float32 [1024], P('chan'), may hold values from 0.25 to 1.75
- reduce_bias: float32 [1024], P('chan'), may hold values from -0.5 to 0.5
- spatial_weight: bfloat16 [3, 3, 1024, 1024], P(None, None, None, 'chan'), may hold values from -0.0625 to 0.0625
- spatial_gain: float32 [1024], P('chan'), may hold values from 0.25 to 1.75
- spatial_bias: float32 [1024], P('chan'), may hold values from -0.5 to 0.5
- expand_weight: bfloat16 [1024, 4096], P(None, 'chan'), may hold values from -0.1875 to 0.1875
- expand_gain: float32 [4096], P('chan'), may hold values from 0.25 to 1.75
- expand_bias: float32 [4096], P('chan'), may hold values from -0.5 to 0.5
Outputs:
- block_out: bfloat16 [64, 14, 14, 4096], P('batch', None, None, 'chan')
Inputs may be any that keep to these rules, and one draw needn't show every extreme that they name: In the images, the per-channel mean and scale differ from one block of 8 images to the next.
All inputs are finite; a program needn't handle non-finite values.
Results may differ from a plain program's by a relative error of at most 0.0047.
Values may be sent and summed in bfloat16 or wider, within the bound.
A program may use at most 128 MiB of HBM per device.

v0:
```python
import functools

import jax
import jax.numpy as jnp
from jax import lax
from jax.experimental import pallas as pl
from jax.experimental.pallas import tpu as pltpu
from jax.sharding import PartitionSpec as P

eps = 0.001
MESH = pl.DeviceIdType.MESH
LIMIT = 63 * 1024 * 1024
SKEW = 3


def remote(src, dst, send, recv, device):
    return pltpu.make_async_remote_copy(
        src_ref=src, dst_ref=dst, send_sem=send, recv_sem=recv,
        device_id=device, device_id_type=MESH,
    )


def greet(n, nb, z, b):
    barrier = pltpu.get_barrier_semaphore()
    for off in range(1, n):
        pl.semaphore_signal(
            barrier, inc=1, device_id={"chan": lax.rem(z + off, n)}, device_id_type=MESH
        )
    for off in range(1, nb):
        pl.semaphore_signal(
            barrier, inc=1, device_id={"batch": lax.rem(b + off, nb)}, device_id_type=MESH
        )
    pl.semaphore_wait(barrier, n + nb - 2)


def share_stats(nb, b, stat_in, send, recv):
    for off in range(1, nb):
        peer = lax.rem(b + off, nb)
        remote(
            stat_in.at[b], stat_in.at[b], send.at[off], recv.at[b], {"batch": peer}
        ).start()
    for off in range(1, nb):
        peer = lax.rem(b + off, nb)
        remote(
            stat_in.at[b], stat_in.at[peer], send.at[off], recv.at[peer], {"batch": peer}
        ).wait()


def combine(stats, local):
    nb = stats.shape[0]
    means = stats[..., 0:1, :]
    mean = jnp.sum(means, axis=0) / nb
    away = means - mean[None]
    spread = jnp.sum(stats[..., 1:2, :], axis=0) + local * jnp.sum(away * away, axis=0)
    return mean, spread / (local * nb)


def first_kernel(
    n, nb, parts, img_hbm, w_ref, gain_ref, bias_ref, out_ref,
    img_ref, img_sem, wown, part, pre_in, suf_in, pre_out, suf_out, gb_in, shift, acc1, acc2, stat_in,
    w1_send, w1_recv, w2_send, w2_recv, w3_send, w3_recv, gb_send, gb_recv,
    pre_send, pre_recv, suf_send, suf_recv, st_send, st_recv,
):
    z, b = lax.axis_index("chan"), lax.axis_index("batch")
    depth = img_ref.shape[2]
    height = img_ref.shape[1]
    strip = depth // nb
    half = nb // 2
    chunks = n * parts
    partner = b + 1 - 2 * lax.rem(b, 2)
    parity = lax.rem(b, 2)
    img_load = pltpu.make_async_copy(img_hbm, img_ref, img_sem)
    img_load.start()
    gb_in[z, 0:1, :] = gain_ref[...]
    gb_in[z, 1:2, :] = bias_ref[...]
    greet(n, nb, z, b)

    def rows_of(who):
        return pl.ds(pl.multiple_of(who * strip, 16), strip)

    for off in range(1, n):
        to = lax.rem(z + off, n)
        src = w_ref.at[pl.ds(pl.multiple_of(to * depth + b * strip, 16), strip), :]
        remote(
            src, wown.at[z, rows_of(b), :], w1_send.at[off], w1_recv.at[z], {"chan": to}
        ).start()
    for off in range(1, n):
        to = lax.rem(z + off, n)
        remote(gb_in.at[z], gb_in.at[z], gb_send.at[off], gb_recv.at[z], {"chan": to}).start()

    wown[z] = w_ref[pl.ds(pl.multiple_of(z * depth, 16), depth), :]

    @pl.when(z == 0)
    def _():
        pre_in[...] = jnp.zeros_like(pre_in)

    @pl.when(z == n - 1)
    def _():
        suf_in[...] = jnp.zeros_like(suf_in)

    def strip_copy(g, who, send, recv, device):
        ref = wown.at[g, rows_of(who), :]
        return remote(ref, ref, send, recv, device)

    for g in range(n):

        @pl.when(z != g)
        def _():
            strip_copy(g, b, w1_send.at[0], w1_recv.at[g], {"chan": g}).wait_recv()
            for hop in range(1, half):
                peer = lax.rem(b + 2 * hop, nb)
                strip_copy(g, b, w2_send.at[g, hop], w2_recv.at[g, b], {"batch": peer}).start()
            strip_copy(g, b, w3_send.at[g, 0], w3_recv.at[g, b], {"batch": partner}).start()

    def forward(g):
        @pl.when(z != g)
        def _():
            for hop in range(1, half):
                peer = lax.rem(b + 2 * hop, nb)
                strip_copy(
                    g, peer, w2_send.at[g, 0], w2_recv.at[g, peer], {"batch": peer}
                ).wait_recv()
                strip_copy(
                    g, peer, w3_send.at[g, hop], w3_recv.at[g, peer], {"batch": partner}
                ).start()

    def complete(g):
        @pl.when(z != g)
        def _():
            for hop in range(half):
                who = 2 * hop + 1 - parity
                strip_copy(
                    g, who, w3_send.at[g, 0], w3_recv.at[g, who], {"batch": partner}
                ).wait_recv()

    forward(0)
    img_load.wait()

    def right_copy(k):
        return remote(
            pre_out.at[k], pre_in.at[k], pre_send.at[k], pre_recv.at[k],
            {"chan": lax.rem(z + 1, n)},
        )

    def left_copy(k):
        return remote(
            suf_out.at[k], suf_in.at[k], suf_send.at[k], suf_recv.at[k],
            {"chan": lax.rem(z + n - 1, n)},
        )

    def step(s, carry):
        @pl.when(s < chunks)
        def _():
            g, r = lax.div(s, parts), lax.rem(s, parts)

            @pl.when(r == 0)
            def _():
                complete(g)

            @pl.when(jnp.logical_and(r == parts // 2, g < n - 1))
            def _():
                forward(g + 1)

            part[s] = jnp.dot(img_ref[r], wown[g], preferred_element_type=jnp.float32)

        kp = s - SKEW * z

        @pl.when(jnp.logical_and(kp >= 0, kp < chunks))
        def _():
            @pl.when(z > 0)
            def _():
                right_copy(kp).wait_recv()

            @pl.when(z < n - 1)
            def _():
                pre_out[kp] = (part[kp] + pre_in[kp].astype(jnp.float32)).astype(jnp.bfloat16)
                right_copy(kp).start()

        ks = s - SKEW * (n - 1 - z)

        @pl.when(jnp.logical_and(ks >= 0, ks < chunks))
        def _():
            @pl.when(z < n - 1)
            def _():
                left_copy(ks).wait_recv()

            @pl.when(z > 0)
            def _():
                suf_out[ks] = (part[ks] + suf_in[ks].astype(jnp.float32)).astype(jnp.bfloat16)
                left_copy(ks).start()

        kf = s - SKEW * jnp.maximum(z, n - 1 - z)

        @pl.when(jnp.logical_and(kf >= 0, kf < chunks))
        def _():
            g, r = lax.div(kf, parts), lax.rem(kf, parts)
            value = (
                part[kf] + pre_in[kf].astype(jnp.float32) + suf_in[kf].astype(jnp.float32)
            )
            part[kf] = value

            @pl.when(r == 0)
            def _():
                shift[g] = jnp.sum(value, axis=0, keepdims=True) / height
                acc1[g] = jnp.zeros_like(acc1[g])
                acc2[g] = jnp.zeros_like(acc2[g])

            moved = value - shift[g]
            acc1[g] += jnp.sum(moved, axis=0, keepdims=True)
            acc2[g] += jnp.sum(moved * moved, axis=0, keepdims=True)

        return carry

    lax.fori_loop(0, chunks + SKEW * (n - 1), step, 0)

    local = height * parts
    extra = acc1[...] / local
    stat_in[b, :, 0:1, :] = shift[...] + extra
    stat_in[b, :, 1:2, :] = acc2[...] - acc1[...] * extra
    share_stats(nb, b, stat_in, st_send, st_recv)
    for off in range(1, n):
        g = lax.rem(z + off, n)
        remote(gb_in.at[z], gb_in.at[g], gb_send.at[off], gb_recv.at[g], {"chan": g}).wait()
    mean, var = combine(stat_in[...], local)
    scale = gb_in[:, 0:1, :] / jnp.sqrt(var + eps)
    bias = gb_in[:, 1:2, :]
    width = part.shape[2]

    def finish(r, carry):
        for g in range(n):
            value = (part[g * parts + r] - mean[g]) * scale[g] + bias[g]
            out_ref[r, :, g * width : (g + 1) * width] = jnp.maximum(value, 0.0).astype(
                jnp.bfloat16
            )
        return carry

    lax.fori_loop(0, parts, finish, 0)

    for off in range(1, n):
        to = lax.rem(z + off, n)
        src = w_ref.at[pl.ds(pl.multiple_of(to * depth + b * strip, 16), strip), :]
        remote(
            src, wown.at[z, rows_of(b), :], w1_send.at[off], w1_recv.at[z], {"chan": to}
        ).wait_send()
        g = to
        for hop in range(1, half):
            peer = lax.rem(b + 2 * hop, nb)
            strip_copy(g, b, w2_send.at[g, hop], w2_recv.at[g, b], {"batch": peer}).wait_send()
        for hop in range(half):
            peer = lax.rem(b + 2 * hop, nb)
            strip_copy(
                g, peer, w3_send.at[g, hop], w3_recv.at[g, peer], {"batch": partner}
            ).wait_send()

    def drain(k, carry):
        @pl.when(z < n - 1)
        def _():
            right_copy(k).wait_send()

        @pl.when(z > 0)
        def _():
            left_copy(k).wait_send()

        return carry

    lax.fori_loop(0, chunks, drain, 0)


def third_kernel(
    n, nb, imgs, one_ref, sw_hbm, mid_gain, mid_bias, w_hbm, gain_ref, out_ref, mean_ref, scale_ref,
    sw_ref, w_ref, sw_sem, w_sem, pad, act, shift, acc1, acc2, stat2, affine, stat3,
    right_send, left_send, recv, s2_send, s2_recv, af_send, af_recv, s3_send, s3_recv,
):
    z, b = lax.axis_index("chan"), lax.axis_index("batch")
    side, height, mid = one_ref.shape
    parts, tall, width = act.shape[1:]
    join = side // parts
    local = parts * tall
    sw_load = pltpu.make_async_copy(sw_hbm, sw_ref, sw_sem)
    sw_load.start()
    w_load = pltpu.make_async_copy(w_hbm, w_ref, w_sem)
    w_load.start()
    pad[:, 0] = jnp.zeros_like(pad[:, 0])
    pad[:, side + 1] = jnp.zeros_like(pad[:, 0])

    def spread(r, carry):
        row = one_ref[r]
        wide = row.astype(jnp.float32)
        edge = jnp.zeros((imgs, mid), jnp.float32)
        pad[1, r + 1] = row
        pad[0, r + 1] = jnp.concatenate([edge, wide[:-imgs]], axis=0).astype(jnp.bfloat16)
        pad[2, r + 1] = jnp.concatenate([wide[imgs:], edge], axis=0).astype(jnp.bfloat16)
        return carry

    lax.fori_loop(0, side, spread, 0)
    acc1[...] = jnp.zeros_like(acc1)
    acc2[...] = jnp.zeros_like(acc2)
    greet(n, nb, z, b)
    sw_load.wait()
    w_load.wait()

    def right_copy(g, r):
        ref = act.at[g, r]
        return remote(
            ref, ref, right_send.at[g, r], recv.at[g, r], {"chan": lax.rem(z + 1, n)}
        )

    def left_copy(g, r):
        ref = act.at[g, r]
        return remote(
            ref, ref, left_send.at[g, r], recv.at[g, r], {"chan": lax.rem(z + n - 1, n)}
        )

    def rows_of(g):
        return pl.ds(pl.multiple_of(g * width, 128), width)

    def convolve(r, carry):
        total = jnp.zeros((tall, width), jnp.float32)
        for row_tap in range(3):
            for col_tap in range(3):
                window = pad[col_tap, pl.ds(r * join + row_tap, join)].reshape(tall, mid)
                total = total + jnp.dot(
                    window, sw_ref[row_tap, col_tap], preferred_element_type=jnp.float32
                )

        @pl.when(r == 0)
        def _():
            shift[...] = jnp.sum(total, axis=0, keepdims=True) / tall

        moved = total - shift[...]
        acc1[...] += jnp.sum(moved, axis=0, keepdims=True)
        acc2[...] += jnp.sum(moved * moved, axis=0, keepdims=True)
        act[z, r] = moved.astype(jnp.bfloat16)

        @pl.when(z < n - 1)
        def _():
            right_copy(z, r).start()

        @pl.when(z > 0)
        def _():
            left_copy(z, r).start()

        return carry

    lax.fori_loop(0, parts, convolve, 0)
    extra = acc1[...] / local
    stat2[b, 0:1, :] = shift[...] + extra
    stat2[b, 1:2, :] = acc2[...] - acc1[...] * extra
    share_stats(nb, b, stat2, s2_send, s2_recv)
    mean, var = combine(stat2[...], local)
    scale = mid_gain[...] / jnp.sqrt(var + eps)
    affine[z, 0:1, :] = scale
    affine[z, 1:2, :] = (shift[...] - mean) * scale + mid_bias[...]

    def affine_copy(off, slot):
        to = lax.rem(z + off, n)
        return remote(
            affine.at[z], affine.at[slot], af_send.at[off], af_recv.at[slot], {"chan": to}
        )

    for off in range(1, n):
        affine_copy(off, z).start()
    for off in range(1, n):
        affine_copy(off, lax.rem(z + off, n)).wait()

    def product(g, r):
        value = act[g, r].astype(jnp.float32) * affine[g, 0:1, :] + affine[g, 1:2, :]
        return jnp.dot(
            jnp.maximum(value, 0.0).astype(jnp.bfloat16),
            w_ref[rows_of(g), :],
            preferred_element_type=jnp.float32,
        )

    def relay(s, carry):
        d, r = lax.div(s, parts) + 1, lax.rem(s, parts)
        g, h = z - d, z + d

        @pl.when(g >= 0)
        def _():
            right_copy(g, r).wait_recv()

            @pl.when(z < n - 1)
            def _():
                right_copy(g, r).start()

        @pl.when(h < n)
        def _():
            left_copy(h, r).wait_recv()

            @pl.when(z > 0)
            def _():
                left_copy(h, r).start()

        @pl.when(d == 1)
        def _():
            out_ref[r] = product(z, r)

        @pl.when(g >= 0)
        def _():
            out_ref[r] += product(g, r)

        @pl.when(h < n)
        def _():
            out_ref[r] += product(h, r)

        return carry

    lax.fori_loop(0, parts * (n - 1), relay, 0)

    base = jnp.sum(out_ref[0], axis=0, keepdims=True) / tall

    def add(r, carry):
        moved = out_ref[r] - base
        return (
            carry[0] + jnp.sum(moved, axis=0, keepdims=True),
            carry[1] + jnp.sum(moved * moved, axis=0, keepdims=True),
        )

    zero = jnp.zeros((1, out_ref.shape[2]), jnp.float32)
    one3, two3 = lax.fori_loop(0, parts, add, (zero, zero))
    extra3 = one3 / local
    stat3[b, 0:1, :] = base + extra3
    stat3[b, 1:2, :] = two3 - one3 * extra3
    share_stats(nb, b, stat3, s3_send, s3_recv)
    mean3, var3 = combine(stat3[...], local)
    mean_ref[...] = mean3
    scale_ref[...] = gain_ref[...] / jnp.sqrt(var3 + eps)

    def drain(s, carry):
        g, r = lax.div(s, parts), lax.rem(s, parts)

        @pl.when(jnp.logical_and(z < n - 1, g <= z))
        def _():
            right_copy(g, r).wait_send()

        @pl.when(jnp.logical_and(z > 0, g >= z))
        def _():
            left_copy(g, r).wait_send()

        return carry

    lax.fori_loop(0, n * parts, drain, 0)


def body(
    images,
    reduce_weight,
    reduce_gain,
    reduce_bias,
    spatial_weight,
    spatial_gain,
    spatial_bias,
    expand_weight,
    expand_gain,
    expand_bias,
):
    imgs, side = (images.shape[0], images.shape[1])
    n, nb = lax.axis_size("chan"), lax.axis_size("batch")
    mid_local = reduce_weight.shape[1]
    mid = mid_local * n
    depth = images.shape[3]
    out_local = expand_weight.shape[1]
    parts, height = side, side * imgs
    chunks = n * parts
    dma, f32, bf16 = pltpu.SemaphoreType.DMA, jnp.float32, jnp.bfloat16
    vmem = pl.BlockSpec(memory_space=pltpu.VMEM)
    flat = images.transpose(1, 2, 0, 3).reshape(parts, height, depth)
    act_one = pl.pallas_call(
        functools.partial(first_kernel, n, nb, parts),
        out_shape=jax.ShapeDtypeStruct((parts, height, mid), bf16),
        in_specs=[pl.BlockSpec(memory_space=pl.ANY)] + [vmem] * 3,
        out_specs=vmem,
        scratch_shapes=[
            pltpu.VMEM((parts, height, depth), bf16),
            dma,
            pltpu.VMEM((n, depth, mid_local), bf16),
            pltpu.VMEM((chunks, height, mid_local), f32),
        ]
        + [pltpu.VMEM((chunks, height, mid_local), bf16)] * 4
        + [pltpu.VMEM((n, 2, mid_local), f32)]
        + [pltpu.VMEM((n, 1, mid_local), f32)] * 3
        + [pltpu.VMEM((nb, n, 2, mid_local), f32)]
        + [dma((n,)), dma((n,)), dma((n, nb // 2)), dma((n, nb)), dma((n, nb // 2)), dma((n, nb))]
        + [dma((n,)), dma((n,))]
        + [dma((chunks,))] * 4
        + [dma((nb,)), dma((nb,))],
        compiler_params=pltpu.CompilerParams(
            collective_id=0, has_side_effects=True, vmem_limit_bytes=LIMIT
        ),
        name="first",
    )(flat, reduce_weight, reduce_gain[None, :], reduce_bias[None, :])
    anywhere = pl.BlockSpec(memory_space=pl.ANY)
    join = 2 if side % 2 == 0 else 1
    pieces, tall = side // join, height * join
    third, mean, scale = pl.pallas_call(
        functools.partial(third_kernel, n, nb, imgs),
        out_shape=(
            jax.ShapeDtypeStruct((pieces, tall, out_local), f32),
            jax.ShapeDtypeStruct((1, out_local), f32),
            jax.ShapeDtypeStruct((1, out_local), f32),
        ),
        in_specs=[vmem, anywhere, vmem, vmem, anywhere, vmem],
        out_specs=(vmem, vmem, vmem),
        scratch_shapes=[
            pltpu.VMEM(spatial_weight.shape, bf16),
            pltpu.VMEM(expand_weight.shape, bf16),
            dma,
            dma,
            pltpu.VMEM((3, side + 2, height, mid), bf16),
            pltpu.VMEM((n, pieces, tall, mid_local), bf16),
        ]
        + [pltpu.VMEM((1, mid_local), f32)] * 3
        + [
            pltpu.VMEM((nb, 2, mid_local), f32),
            pltpu.VMEM((n, 2, mid_local), f32),
            pltpu.VMEM((nb, 2, out_local), f32),
        ]
        + [dma((n, pieces))] * 3
        + [dma((nb,))] * 2
        + [dma((n,))] * 2
        + [dma((nb,))] * 2,
        compiler_params=pltpu.CompilerParams(
            collective_id=1, has_side_effects=True, vmem_limit_bytes=LIMIT
        ),
        name="third",
    )(
        act_one,
        spatial_weight,
        spatial_gain[None, :],
        spatial_bias[None, :],
        expand_weight,
        expand_gain[None, :],
    )
    third = third.reshape(side, height, out_local)
    normed = (third - mean[0]) * scale[0] + expand_bias
    out = jnp.maximum(normed + flat.astype(f32), 0.0).astype(bf16)
    return out.reshape(side, side, imgs, out_local).transpose(2, 0, 1, 3)


def solution(mesh):
    in_specs = (
        P("batch", None, None, "chan"),
        P(None, "chan"),
        P("chan"),
        P("chan"),
        P(None, None, None, "chan"),
        P("chan"),
        P("chan"),
        P(None, "chan"),
        P("chan"),
        P("chan"),
    )
    out_specs = P("batch", None, None, "chan")
    return jax.shard_map(body, mesh=mesh, in_specs=in_specs, out_specs=out_specs, check_vma=False)
```

profile of v0, /device:TPU:0, one launch (start us, length us, event | category | flops | bytes accessed | tf_op | source)
XLA Modules:
  0.0 185.3 jit_solution(16690449491027174778)
XLA Ops:
  0.0 107.5 %first.1.one_ref = bf16[14,112,1024]{2,1,0:T(8,128)(2,1)} custom-call(bf16[14,112,1024]{2,1,0:T(8,128)(2,1)} %bitcast.14, bf16[4096,256]{1,0:T(8,128)(2,1)} %w_ref.1, f32[1,256]{1,0:T(1,128)} %bitcast.19, f32[1,256]{1,0:T(1,128)} %bitcast.20), custom_call_target="tpu_custom_call" | custom-call | tf_op jit(solution)/shard_map/first/pallas_call | solution.py:468
  107.5 0.0 copy-start
  107.5 70.8 %third.1 = (f32[7,224,1024]{2,1,0:T(8,128)}, f32[1,1024]{1,0:T(1,128)}, f32[1,1024]{1,0:T(1,128)}) custom-call(bf16[14,112,1024]{2,1,0:T(8,128)(2,1)} %first.1.one_ref, bf16[3,3,1024,256]{3,2,1,0:T(8,128)(2,1)} %sw_hbm.1, f32[1,256]{1,0:T(1,128)} %bitcast.21, f32[1,256]{1,0:T(1,128)} %bitcast.22, bf16[1024,1024]{1,0:T(8,128)(2,1)} %w_hbm.1, f32[1,1024]{1,0:T(1,128)} %bitcast.16), custom_call_target="tpu_custom_call" | custom-call | tf_op jit(solution)/shard_map/third/pallas_call | solution.py:495
  178.3 0.0 copy-done
  178.4 6.9 %fusion = bf16[8,14,14,1024]{3,0,2,1:T(8,128)(2,1)} fusion(f32[14,14,8,1024]{3,2,1,0:T(8,128)} %bitcast.15, bf16[8,14,14,1024]{3,0,2,1:T(8,128)(2,1)} %param.10, f32[1024]{0:T(1024)S(1)} %copy-done, f32[1024]{0:T(1024)} %bitcast.18, f32[1024]{0:T(1024)} %bitcast.17), kind=kLoop, calls=%fused_computation.1 | loop fusion | flops 11239424 | bytes 12857344 | tf_op jit(solution)/shard_map/transpose | solution.py:537
Async XLA Ops:
  107.5 70.9 %copy-start = (f32[1024]{0:T(1024)S(1)}, f32[1024]{0:T(1024)}, u32[]{:S(2)}) copy-start(f32[1024]{0:T(1024)} %param.19) | copy-start | bytes 12292
where the time goes:
time: 185 us
  Pallas kernels  178 us (96%)
  other arithmetic  6.94 us (4%)
    pallas_call x1, Pallas kernels, body(): pl.pallas_call(functools.partial(first_kernel, n, nb, parts), out_shape=j...  107 us
    pallas_call x1, Pallas kernels, body(): pl.pallas_call(functools.partial(third_kernel, n, nb, imgs), out_shape=(j...  70.8 us
    transpose x1, other arithmetic, body(): return out.reshape(side, side, imgs, out_local).transpose(2, 0, 1, 3)  6.94 us

commit v1 on v0

v1 whole, which is shorter than its diff:
```python
import functools

import jax
import jax.numpy as jnp
from jax import lax
from jax.experimental import pallas as pl
from jax.experimental.pallas import tpu as pltpu
from jax.sharding import PartitionSpec as P

eps = 0.001
MESH = pl.DeviceIdType.MESH
LIMIT = 63 * 1024 * 1024
SKEW = 3
SINK = 1
HELD = 3
READY = 12


def remote(src, dst, send, recv, device):
    return pltpu.make_async_remote_copy(
        src_ref=src, dst_ref=dst, send_sem=send, recv_sem=recv,
        device_id=device, device_id_type=MESH,
    )


def greet(n, nb, z, b):
    barrier = pltpu.get_barrier_semaphore()
    for off in range(1, n):
        pl.semaphore_signal(
            barrier, inc=1, device_id={"chan": lax.rem(z + off, n)}, device_id_type=MESH
        )
    for off in range(1, nb):
        pl.semaphore_signal(
            barrier, inc=1, device_id={"batch": lax.rem(b + off, nb)}, device_id_type=MESH
        )
    pl.semaphore_wait(barrier, n + nb - 2)


def stats_send(nb, b, stats, send, recv):
    for off in range(1, nb):
        peer = lax.rem(b + off, nb)
        remote(stats.at[b], stats.at[b], send.at[off], recv.at[b], {"batch": peer}).start()


def stats_wait(nb, b, stats, send, recv):
    for off in range(1, nb):
        peer = lax.rem(b + off, nb)
        remote(stats.at[b], stats.at[peer], send.at[off], recv.at[peer], {"batch": peer}).wait()


def combine(stats, local):
    nb = stats.shape[0]
    means = stats[:, 0:1, :]
    mean = jnp.sum(means, axis=0) / nb
    away = means - mean[None]
    spread = jnp.sum(stats[:, 1:2, :], axis=0) + local * jnp.sum(away * away, axis=0)
    return mean, spread / (local * nb)


def column_sum(value):
    return jnp.sum(value, axis=0, keepdims=True)


def block_kernel(
    n, nb, imgs,
    img_hbm, w1_hbm, gain1, bias1, sw_hbm, gain2, bias2, w3_hbm, gain3, bias3,
    out_hbm,
    img, w1, wown, part, whole, flow, gb, shift1, sum1, square1, stat1, act, w2, acc, sec,
    shift2, sum2, square2, stat2, affine, w3, third, shift3, sum3, square3, stat3, outv,
    load_sem, out_sem,
    gb_send, gb_recv, w1_send, w1_recv, hop_send, hop_recv, pair_send, pair_recv,
    flow_send, flow_recv, st1_send, st1_recv,
    w2_send, w2_recv, w2hop_send, w2hop_recv, w2pair_send, w2pair_recv,
    sec_send, sec_recv, st2_send, st2_recv, aff_send, aff_recv, st3_send, st3_recv,
):
    z, b = lax.axis_index("chan"), lax.axis_index("batch")
    rows, height, depth = img.shape
    width = wown.shape[2]
    half = acc.shape[2]
    pieces, tall, out_local = third.shape
    join = rows // pieces
    mids = n // 2
    hops = nb // 2
    chunks = n * rows
    strip = depth // nb
    band = n * width // nb
    local = rows * height
    unit = half // 2
    per_piece = join * 2
    units = rows * 2
    partner = b + 1 - 2 * lax.rem(b, 2)
    parity = lax.rem(b, 2)
    at_first, at_last = z == 0, z == n - 1
    at_end = jnp.logical_or(at_first, at_last)
    inner = jnp.logical_not(at_end)
    side = jnp.where(at_first, 0, 1)
    owner = jnp.where(z < mids, 0, n - 1)
    my_slot = lax.rem(z, mids)
    f32, bf16 = jnp.float32, jnp.bfloat16

    w1_load = pltpu.make_async_copy(w1_hbm, w1, load_sem.at[0])
    w1_load.start()
    img_load = pltpu.make_async_copy(img_hbm, img, load_sem.at[1])
    img_load.start()
    w3_load = pltpu.make_async_copy(w3_hbm, w3, load_sem.at[2])
    w3_load.start()

    def slot_cols(slot):
        return pl.ds(pl.multiple_of(slot * width, 128), width)

    w2_load = pltpu.make_async_copy(sw_hbm, w2.at[:, :, :, slot_cols(my_slot)], load_sem.at[3])

    @pl.when(at_end)
    def _():
        w2_load.start()

    gb[z, 0:1, :] = gain1[...]
    gb[z, 1:2, :] = bias1[...]
    gb[z, 2:3, :] = gain2[...]
    gb[z, 3:4, :] = bias2[...]
    greet(n, nb, z, b)

    def rows_of(who):
        return pl.ds(pl.multiple_of(who * strip, 16), strip)

    def w1_copy(to):
        src = w1.at[pl.ds(pl.multiple_of(to * depth + b * strip, 16), strip), :]
        return remote(src, wown.at[z, rows_of(b), :], w1_send.at[to], w1_recv.at[z], {"chan": to})

    def gb_copy(to, slot):
        return remote(gb.at[z], gb.at[slot], gb_send.at[to], gb_recv.at[slot], {"chan": to})

    def band_of(who):
        return pl.ds(pl.multiple_of(who * band, 16), band)

    w2_copy = remote(
        sw_hbm.at[:, :, band_of(b), :], w2.at[:, :, band_of(b), slot_cols(my_slot)],
        w2_send.at[0], w2_recv.at[my_slot], {"chan": owner},
    )
    w1_load.wait()
    for far in range(1, n):

        @pl.when(z + far < n)
        def _():
            w1_copy(z + far).start()

        @pl.when(z - far >= 0)
        def _():
            w1_copy(z - far).start()

    for off in range(1, n):
        gb_copy(lax.rem(z + off, n), z).start()

    @pl.when(inner)
    def _():
        w2_copy.start()

    def strip_copy(g, who, send, recv, device):
        ref = wown.at[g, rows_of(who), :]
        return remote(ref, ref, send, recv, device)

    def hop_copy(g, hop):
        peer = lax.rem(b + 2 * hop, nb)
        return strip_copy(g, b, hop_send.at[g, hop], hop_recv.at[g, b], {"batch": peer})

    def pair_copy(g, hop):
        who = lax.rem(b + 2 * hop, nb)
        return strip_copy(g, who, pair_send.at[g, hop], pair_recv.at[g, who], {"batch": partner})

    def distribute(g):
        @pl.when(z != g)
        def _():
            strip_copy(g, b, w1_send.at[0], w1_recv.at[g], {"chan": g}).wait_recv()
            for hop in range(1, hops):
                hop_copy(g, hop).start()
            pair_copy(g, 0).start()

    def forward(g):
        @pl.when(z != g)
        def _():
            for hop in range(1, hops):
                peer = lax.rem(b + 2 * hop, nb)
                strip_copy(
                    g, peer, hop_send.at[g, 0], hop_recv.at[g, peer], {"batch": peer}
                ).wait_recv()
                pair_copy(g, hop).start()

    def complete(g):
        @pl.when(z != g)
        def _():
            for hop in range(hops):
                who = 2 * hop + 1 - parity
                strip_copy(
                    g, who, pair_send.at[g, 0], pair_recv.at[g, who], {"batch": partner}
                ).wait_recv()

    def flow_copy(f, k):
        to = jnp.where(f == 0, lax.rem(z + 1, n), lax.rem(z + n - 1, n))
        ref = flow.at[f, k]
        return remote(ref, ref, flow_send.at[f, k], flow_recv.at[f, k], {"chan": to})

    def chunk_of(f, position):
        q, r = lax.div(position, rows), lax.rem(position, rows)
        return jnp.where(f == 0, q, n - 1 - q) * rows + r

    img_load.wait()

    def own_products(r, carry):
        k = z * rows + r
        value = jnp.dot(
            img[r], w1[pl.ds(pl.multiple_of(z * depth, 16), depth), :], preferred_element_type=f32
        )
        part[k] = value

        @pl.when(at_end)
        def _():
            flow[side, k] = value.astype(bf16)
            flow_copy(side, k).start()

        return carry

    split = rows // 2
    lax.fori_loop(0, split, own_products, 0)
    order = [g for q in range(mids) for g in (q, n - 1 - q)]
    for g in order[:2]:
        distribute(g)
    lax.fori_loop(split, rows, own_products, 0)
    for g in order[2:]:
        distribute(g)
    act[:, 0] = jnp.zeros_like(act[:, 0])
    act[:, rows + 1] = jnp.zeros_like(act[:, 0])
    acc[...] = jnp.zeros_like(acc)
    for g in order[:2]:
        forward(g)

    def band_copy(slot, who, send, recv, device):
        ref = w2.at[:, :, band_of(who), slot_cols(slot)]
        return remote(ref, ref, send, recv, device)

    def w2hop_copy(slot, hop):
        peer = lax.rem(b + 2 * hop, nb)
        return band_copy(slot, b, w2hop_send.at[slot, hop], w2hop_recv.at[slot, b], {"batch": peer})

    def w2pair_copy(slot, hop):
        who = lax.rem(b + 2 * hop, nb)
        return band_copy(
            slot, who, w2pair_send.at[slot, hop], w2pair_recv.at[slot, who], {"batch": partner}
        )

    def each_slot(work):
        for slot in range(mids):

            @pl.when(slot != my_slot)
            def _():
                work(slot)

    def w2_distribute(slot):
        band_copy(slot, b, w2_send.at[0], w2_recv.at[slot], {"chan": z}).wait_recv()
        for hop in range(1, hops):
            w2hop_copy(slot, hop).start()
        w2pair_copy(slot, 0).start()

    def w2_forward(slot):
        for hop in range(1, hops):
            peer = lax.rem(b + 2 * hop, nb)
            band_copy(
                slot, peer, w2hop_send.at[slot, 0], w2hop_recv.at[slot, peer], {"batch": peer}
            ).wait_recv()
            w2pair_copy(slot, hop).start()

    def w2_complete(slot):
        for hop in range(hops):
            who = 2 * hop + 1 - parity
            band_copy(
                slot, who, w2pair_send.at[slot, 0], w2pair_recv.at[slot, who], {"batch": partner}
            ).wait_recv()

    def end_group(q):
        return jnp.where(at_first, n - 1 - q, q)

    def finalize(position):
        f = 1 - side
        k = chunk_of(f, position)
        g, r = lax.div(k, rows), lax.rem(k, rows)
        flow_copy(f, k).wait_recv()
        value = part[k] + flow[f, k].astype(f32)
        whole[lax.rem(lax.div(position, rows), 2), r] = value

        @pl.when(r == 0)
        def _():
            shift1[g] = column_sum(value) / height
            sum1[g] = jnp.zeros_like(sum1[g])
            square1[g] = jnp.zeros_like(square1[g])

        moved = value - shift1[g]
        sum1[g] += column_sum(moved)
        square1[g] += column_sum(moved * moved)

    def first_stats(g):
        extra = sum1[g] / local
        stat1[g, b, 0:1, :] = shift1[g] + extra
        stat1[g, b, 1:2, :] = square1[g] - sum1[g] * extra
        stats_send(nb, b, stat1.at[g], st1_send.at[g], st1_recv.at[g])

    def first_act(q):
        g = end_group(q)
        stats_wait(nb, b, stat1.at[g], st1_send.at[g], st1_recv.at[g])
        mean, var = combine(stat1[g], local)
        scale = gb[g, 0:1, :] / jnp.sqrt(var + eps)
        bias = gb[g, 1:2, :]

        def line(r, carry):
            value = (whole[lax.rem(q, 2), r] - mean) * scale + bias
            act[g, r + 1] = jnp.maximum(value, 0.0).astype(bf16)
            return carry

        lax.fori_loop(0, rows, line, 0)

    def convolve(g, t):
        for col_tap in range(3):
            total = None
            for row_tap in range(3):
                window = act[g, pl.ds(t * join + row_tap, join)].reshape(tall, width)
                weight = w2[row_tap, col_tap, pl.ds(pl.multiple_of(g * width, 128), width), :]
                term = jnp.dot(window, weight, preferred_element_type=f32)
                total = term if total is None else total + term
            total = total.reshape(join, height, half)
            lines = pl.ds(t * join, join)
            if col_tap == 0:
                acc[lines, imgs:, :] += total[:, : height - imgs]
            elif col_tap == 1:
                acc[lines] += total
            else:
                acc[lines, : height - imgs, :] += total[:, imgs:]

    reach = SKEW * (n - 1) + SINK

    def step(s, carry):
        q, r = lax.div(s, rows), lax.rem(s, rows)

        @pl.when(q < mids)
        def _():
            @pl.when(r == 0)
            def _():
                complete(q)
                complete(n - 1 - q)

            @pl.when(jnp.logical_and(r == rows // 2, q + 1 < mids))
            def _():
                forward(q + 1)
                forward(n - 2 - q)

            for g in (q, n - 1 - q):

                @pl.when(z != g)
                def _():
                    part[g * rows + r] = jnp.dot(img[r], wown[g], preferred_element_type=f32)

        for f in range(2):
            from_start = z if f == 0 else n - 1 - z
            position = s - SKEW * from_start
            k = chunk_of(f, position)
            inside = jnp.logical_and(position >= 0, position < chunks)

            @pl.when(jnp.logical_and(inside, jnp.logical_and(from_start == 0, position >= rows)))
            def _():
                flow[f, k] = part[k].astype(bf16)
                flow_copy(f, k).start()

            @pl.when(jnp.logical_and(inside, inner))
            def _():
                flow_copy(f, k).wait_recv()
                flow[f, k] = (part[k] + flow[f, k].astype(f32)).astype(bf16)
                flow_copy(f, k).start()

        @pl.when(at_end)
        def _():
            @pl.when(s == rows // 2)
            def _():
                each_slot(w2_distribute)

            @pl.when(s == rows + rows // 2)
            def _():
                each_slot(w2_forward)

            position = s - reach

            @pl.when(position >= 0)
            def _():
                finalize(position)

            after = position - (rows - 1)

            @pl.when(after >= 0)
            def _():
                q, v = lax.div(after, rows), lax.rem(after, rows)
                g = end_group(q)

                @pl.when(v == 0)
                def _():
                    first_stats(g)

                @pl.when(v == 4)
                def _():
                    @pl.when(q == 0)
                    def _():
                        for to in range(n):

                            @pl.when(z != to)
                            def _():
                                gb_copy(to, to).wait_recv()

                        w2_load.wait()
                        each_slot(w2_complete)

                    first_act(q)

                @pl.when(jnp.logical_and(v >= 5, v < 5 + pieces))
                def _():
                    convolve(g, v - 5)

        return carry

    lax.fori_loop(0, chunks + reach, step, 0)

    def sec_copy(f, u):
        to = jnp.where(f == 0, lax.rem(z + 1, n), lax.rem(z + n - 1, n))
        line, part_of = lax.div(u, 2), lax.rem(u, 2)
        ref = sec.at[f, line, :, pl.ds(pl.multiple_of(part_of * unit, 128), unit)]
        return remote(ref, ref, sec_send.at[f, u], sec_recv.at[f, u], {"chan": to})

    def sec_start(u, carry):
        sec_copy(side, u).start()
        return carry

    def affine_copy(to, f):
        return remote(affine.at[f], affine.at[f], aff_send.at[to], aff_recv.at[f], {"chan": to})

    @pl.when(at_end)
    def _():
        last = end_group(n - 1)
        first_act(n - 1)
        sum2[...] = jnp.zeros_like(sum2)
        square2[...] = jnp.zeros_like(square2)

        def tail(t, carry):
            convolve(last, t)
            lines = pl.ds(t * join, join)
            total = acc[lines].reshape(tall, half)

            @pl.when(t == 0)
            def _():
                shift2[...] = column_sum(total) / tall

            moved = total - shift2[...]
            sum2[...] += column_sum(moved)
            square2[...] += column_sum(moved * moved)
            sec[side, lines] = moved.astype(bf16).reshape(join, height, half)

            @pl.when(t < HELD)
            def _():
                lax.fori_loop(t * per_piece, (t + 1) * per_piece, sec_start, 0)

            return carry

        lax.fori_loop(0, pieces, tail, 0)
        extra = sum2[...] / local
        stat2[b, 0:1, :] = shift2[...] + extra
        stat2[b, 1:2, :] = square2[...] - sum2[...] * extra
        stats_send(nb, b, stat2, st2_send, st2_recv)
        stats_wait(nb, b, stat2, st2_send, st2_recv)
        mean, var = combine(stat2[...], local)
        inverse = 1.0 / jnp.sqrt(var + eps)
        for i in range(mids):
            cols = slice(i * width, (i + 1) * width)
            block = side * mids + i
            scale = gb[block, 2:3, :] * inverse[:, cols]
            affine[side, 0:1, cols] = scale
            affine[side, 1:2, cols] = (shift2[:, cols] - mean[:, cols]) * scale + gb[block, 3:4, :]
        for off in range(1, n):
            affine_copy(lax.rem(z + off, n), side).start()
        lax.fori_loop(min(HELD, pieces) * per_piece, units, sec_start, 0)

    w3_load.wait()
    sum3[...] = jnp.zeros_like(sum3)
    square3[...] = jnp.zeros_like(square3)
    lag = SKEW * jnp.maximum(z - 1, n - 2 - z)

    def expand(t):
        total = None
        for f in range(2):
            value = sec[f, pl.ds(t * join, join)].reshape(tall, half).astype(f32)
            value = value * affine[f, 0:1, :] + affine[f, 1:2, :]
            term = jnp.dot(
                jnp.maximum(value, 0.0).astype(bf16), w3[f * half : (f + 1) * half, :],
                preferred_element_type=f32,
            )
            total = term if total is None else total + term
        third[t] = total

        @pl.when(t == 0)
        def _():
            shift3[...] = column_sum(total) / tall

        moved = third[t] - shift3[...]
        sum3[...] += column_sum(moved)
        square3[...] += column_sum(moved * moved)

    def relay(s, carry):
        for f in range(2):
            gone = z - 1 if f == 0 else n - 2 - z
            position = s - SKEW * gone

            @pl.when(jnp.logical_and(gone >= 0, jnp.logical_and(position >= 0, position < units)))
            def _():
                sec_copy(f, position).wait_recv()

                @pl.when(inner)
                def _():
                    sec_copy(f, position).start()

        @pl.when(s == READY)
        def _():
            for f in range(2):

                @pl.when(z != f * (n - 1))
                def _():
                    affine_copy(f * (n - 1), f).wait_recv()

        late = s - READY
        t_late = lax.div(late, 2)
        catching = jnp.logical_and(late >= 0, lax.rem(late, 2) == 0)
        catching = jnp.logical_and(catching, t_late < pieces)
        catching = jnp.logical_and(catching, per_piece * (t_late + 1) - 1 + lag <= s)
        fresh = s - (per_piece - 1) - lag
        t_fresh = lax.div(fresh, per_piece)
        arriving = jnp.logical_and(fresh >= 0, lax.rem(fresh, per_piece) == 0)
        arriving = jnp.logical_and(arriving, t_fresh < pieces)
        arriving = jnp.logical_and(arriving, READY + 2 * t_fresh < s)

        @pl.when(jnp.logical_or(catching, arriving))
        def _():
            expand(jnp.where(catching, t_late, t_fresh))

        return carry

    relay_steps = max(units + SKEW * (n - 2), READY + 2 * pieces)
    lax.fori_loop(0, relay_steps, relay, 0)

    extra = sum3[...] / local
    stat3[b, 0:1, :] = shift3[...] + extra
    stat3[b, 1:2, :] = square3[...] - sum3[...] * extra
    stats_send(nb, b, stat3, st3_send, st3_recv)

    for to in range(n):

        @pl.when(z != to)
        def _():
            w1_copy(to).wait_send()
            gb_copy(to, z).wait_send()
            for hop in range(1, hops):
                hop_copy(to, hop).wait_send()
            for hop in range(hops):
                pair_copy(to, hop).wait_send()

            @pl.when(inner)
            def _():
                gb_copy(to, to).wait_recv()

            @pl.when(at_end)
            def _():
                affine_copy(to, side).wait_send()

    @pl.when(inner)
    def _():
        w2_copy.wait_send()

    def w2_drain(slot):
        for hop in range(1, hops):
            w2hop_copy(slot, hop).wait_send()
        for hop in range(hops):
            w2pair_copy(slot, hop).wait_send()

    @pl.when(at_end)
    def _():
        each_slot(w2_drain)

    for f in range(2):

        @pl.when(z != (n - 1) * (1 - f))
        def _():
            def drain_flow(k, carry):
                flow_copy(f, k).wait_send()
                return carry

            def drain_sec(u, carry):
                sec_copy(f, u).wait_send()
                return carry

            lax.fori_loop(0, chunks, drain_flow, 0)
            lax.fori_loop(0, units, drain_sec, 0)

    stats_wait(nb, b, stat3, st3_send, st3_recv)
    mean3, var3 = combine(stat3[...], local)
    scale3 = gain3[...] / jnp.sqrt(var3 + eps)
    bias3_value = bias3[...]

    def out_copy(t):
        return pltpu.make_async_copy(outv.at[t], out_hbm.at[t], out_sem.at[t])

    def finish(t, carry):
        kept = img[pl.ds(t * join, join)].reshape(tall, out_local).astype(f32)
        value = (third[t] - mean3) * scale3 + bias3_value + kept
        outv[t] = jnp.maximum(value, 0.0).astype(bf16)
        out_copy(t).start()
        return carry

    lax.fori_loop(0, pieces, finish, 0)

    def out_drain(t, carry):
        out_copy(t).wait()
        return carry

    lax.fori_loop(0, pieces, out_drain, 0)


def body(
    images,
    reduce_weight,
    reduce_gain,
    reduce_bias,
    spatial_weight,
    spatial_gain,
    spatial_bias,
    expand_weight,
    expand_gain,
    expand_bias,
):
    imgs, side = (images.shape[0], images.shape[1])
    n, nb = lax.axis_size("chan"), lax.axis_size("batch")
    width = reduce_weight.shape[1]
    depth = images.shape[3]
    out_local = expand_weight.shape[1]
    rows, height = side, side * imgs
    chunks = n * rows
    mid = n * width
    half = mid // 2
    mids = n // 2
    join = 2 if side % 2 == 0 else 1
    pieces, tall = side // join, height * join
    dma, f32, bf16 = pltpu.SemaphoreType.DMA, jnp.float32, jnp.bfloat16
    vmem = pl.BlockSpec(memory_space=pltpu.VMEM)
    anywhere = pl.BlockSpec(memory_space=pl.ANY)
    flat = images.transpose(1, 2, 0, 3).reshape(rows, height, depth)
    out = pl.pallas_call(
        functools.partial(block_kernel, n, nb, imgs),
        out_shape=jax.ShapeDtypeStruct((pieces, tall, out_local), bf16),
        in_specs=[anywhere, anywhere, vmem, vmem, anywhere, vmem, vmem, anywhere, vmem, vmem],
        out_specs=anywhere,
        scratch_shapes=[
            pltpu.VMEM((rows, height, depth), bf16),
            pltpu.VMEM(reduce_weight.shape, bf16),
            pltpu.VMEM((n, depth, width), bf16),
            pltpu.VMEM((chunks, height, width), f32),
            pltpu.VMEM((2, rows, height, width), f32),
            pltpu.VMEM((2, chunks, height, width), bf16),
            pltpu.VMEM((n, 4, width), f32),
        ]
        + [pltpu.VMEM((n, 1, width), f32)] * 3
        + [
            pltpu.VMEM((n, nb, 2, width), f32),
            pltpu.VMEM((n, rows + 2, height, width), bf16),
            pltpu.VMEM((3, 3, mid, half), bf16),
            pltpu.VMEM((rows, height, half), f32),
            pltpu.VMEM((2, rows, height, half), bf16),
        ]
        + [pltpu.VMEM((1, half), f32)] * 3
        + [
            pltpu.VMEM((nb, 2, half), f32),
            pltpu.VMEM((2, 2, half), f32),
            pltpu.VMEM(expand_weight.shape, bf16),
            pltpu.VMEM((pieces, tall, out_local), f32),
        ]
        + [pltpu.VMEM((1, out_local), f32)] * 3
        + [pltpu.VMEM((nb, 2, out_local), f32), pltpu.VMEM((pieces, tall, out_local), bf16)]
        + [dma((4,)), dma((pieces,))]
        + [dma((n,))] * 4
        + [dma((n, nb // 2)), dma((n, nb))] * 2
        + [dma((2, chunks))] * 2
        + [dma((n, nb))] * 2
        + [dma((1,)), dma((mids,))]
        + [dma((mids, nb // 2)), dma((mids, nb))] * 2
        + [dma((2, 2 * rows))] * 2
        + [dma((nb,))] * 2
        + [dma((n,)), dma((2,))]
        + [dma((nb,))] * 2,
        compiler_params=pltpu.CompilerParams(
            collective_id=0, has_side_effects=True, vmem_limit_bytes=LIMIT
        ),
        name="block",
    )(
        flat,
        reduce_weight,
        reduce_gain[None, :],
        reduce_bias[None, :],
        spatial_weight,
        spatial_gain[None, :],
        spatial_bias[None, :],
        expand_weight,
        expand_gain[None, :],
        expand_bias[None, :],
    )
    return out.reshape(side, side, imgs, out_local).transpose(2, 0, 1, 3)


def solution(mesh):
    in_specs = (
        P("batch", None, None, "chan"),
        P(None, "chan"),
        P("chan"),
        P("chan"),
        P(None, None, None, "chan"),
        P("chan"),
        P("chan"),
        P(None, "chan"),
        P("chan"),
        P("chan"),
    )
    out_specs = P("batch", None, None, "chan")
    return jax.shard_map(body, mesh=mesh, in_specs=in_specs, out_specs=out_specs, check_vma=False)
```

time: 185 us -> 166 us (0.90)
  Pallas kernels: 178 us -> 162 us
  other arithmetic: 6.94 us -> 0 us
  local copies, waits for them, and re-layouts: 0.01 us -> 3.96 us
    pallas_call x2 -> x1, Pallas kernels: 178 us -> 162 us  [body(): pl.pallas_call(functools.partial(block_kernel, n, nb, imgs), out_shape=ja...]
    transpose x1 -> x0, other arithmetic: 6.94 us -> none  [body(): return out.reshape(side, side, imgs, out_local).transpose(2, 0, 1, 3)]
    unnamed x2 -> x1, local copies, waits for them, and re-layouts: 0.01 us -> 3.96 us
where the time goes in v1:
time: 166 us
  Pallas kernels  162 us (98%)
  local copies, waits for them, and re-layouts  3.96 us (2%)
    pallas_call x1, Pallas kernels, body(): pl.pallas_call(functools.partial(block_kernel, n, nb, imgs), out_shape=ja...  162 us
    unnamed x1, local copies, waits for them, and re-layouts  3.96 us

profile of v1, /device:TPU:0, one launch (start us, length us, event | category | flops | bytes accessed | tf_op | source)
XLA Modules:
  0.0 166.1 jit_solution(9287920036443693560)
XLA Ops:
  0.0 162.1 %block.1 = bf16[7,224,1024]{2,1,0:T(8,128)(2,1)} custom-call(bf16[14,112,1024]{2,1,0:T(8,128)(2,1)} %bitcast.13, bf16[4096,256]{1,0:T(8,128)(2,1)} %w1_hbm.1, f32[1,256]{1,0:T(1,128)} %bitcast.16, f32[1,256]{1,0:T(1,128)} %bitcast.17, bf16[3,3,1024,256]{3,2,1,0:T(8,128)(2,1)} %sw_hbm.1, f32[1,256]{1,0:T(1,128)} %bitcast.18, f32[1,256]{1,0:T(1,128)} %bitcast.19, ...), custom_call_target="tpu_custom_call" | custom-call | tf_op jit(solution)/shard_map/block/pallas_call | solution.py:655
  162.2 4.0 %copy.12 = bf16[8,14,14,1024]{3,0,2,1:T(8,128)(2,1)} copy(bf16[8,14,14,1024]{3,0,2,1:T(8,128)(2,1)} %bitcast.12) | data formatting | bytes 6422528

commit v2 on v1

--- a/solution.py
+++ b/solution.py
@@ -9,11 +9,12 @@
 
 eps = 0.001
 MESH = pl.DeviceIdType.MESH
-LIMIT = 63 * 1024 * 1024
+LIMIT = 59 * 1024 * 1024
 SKEW = 3
 SINK = 1
-HELD = 3
-READY = 12
+HELD = 2
+READY = 11
+LAG = 5
 
 
 def remote(src, dst, send, recv, device):
@@ -39,13 +40,12 @@
 def stats_send(nb, b, stats, send, recv):
     for off in range(1, nb):
         peer = lax.rem(b + off, nb)
-        remote(stats.at[b], stats.at[b], send.at[off], recv.at[b], {"batch": peer}).start()
+        remote(stats.at[b], stats.at[b], send, recv, {"batch": peer}).start()
 
 
 def stats_wait(nb, b, stats, send, recv):
-    for off in range(1, nb):
-        peer = lax.rem(b + off, nb)
-        remote(stats.at[b], stats.at[peer], send.at[off], recv.at[peer], {"batch": peer}).wait()
+    others = stats.at[pl.ds(0, nb - 1)]
+    remote(others, others, send, recv, {"batch": lax.rem(b + 1, nb)}).wait()
 
 
 def combine(stats, local):
@@ -64,10 +64,10 @@
 def block_kernel(
     n, nb, imgs,
     img_hbm, w1_hbm, gain1, bias1, sw_hbm, gain2, bias2, w3_hbm, gain3, bias3,
-    out_hbm,
+    outv,
     img, w1, wown, part, whole, flow, gb, shift1, sum1, square1, stat1, act, w2, acc, sec,
-    shift2, sum2, square2, stat2, affine, w3, third, shift3, sum3, square3, stat3, outv,
-    load_sem, out_sem,
+    shift2, sum2, square2, stat2, affine, w3, third, shift3, sum3, square3, stat3,
+    load_sem,
     gb_send, gb_recv, w1_send, w1_recv, hop_send, hop_recv, pair_send, pair_recv,
     flow_send, flow_recv, st1_send, st1_recv,
     w2_send, w2_recv, w2hop_send, w2hop_recv, w2pair_send, w2pair_recv,
@@ -125,10 +125,10 @@
 
     def w1_copy(to):
         src = w1.at[pl.ds(pl.multiple_of(to * depth + b * strip, 16), strip), :]
-        return remote(src, wown.at[z, rows_of(b), :], w1_send.at[to], w1_recv.at[z], {"chan": to})
+        return remote(src, wown.at[z, rows_of(b), :], w1_send.at[0], w1_recv.at[z], {"chan": to})
 
     def gb_copy(to, slot):
-        return remote(gb.at[z], gb.at[slot], gb_send.at[to], gb_recv.at[slot], {"chan": to})
+        return remote(gb.at[z], gb.at[slot], gb_send.at[0], gb_recv.at[0], {"chan": to})
 
     def band_of(who):
         return pl.ds(pl.multiple_of(who * band, 16), band)
@@ -159,45 +159,40 @@
         ref = wown.at[g, rows_of(who), :]
         return remote(ref, ref, send, recv, device)
 
-    def hop_copy(g, hop):
-        peer = lax.rem(b + 2 * hop, nb)
-        return strip_copy(g, b, hop_send.at[g, hop], hop_recv.at[g, b], {"batch": peer})
-
-    def pair_copy(g, hop):
-        who = lax.rem(b + 2 * hop, nb)
-        return strip_copy(g, who, pair_send.at[g, hop], pair_recv.at[g, who], {"batch": partner})
-
     def distribute(g):
         @pl.when(z != g)
         def _():
             strip_copy(g, b, w1_send.at[0], w1_recv.at[g], {"chan": g}).wait_recv()
             for hop in range(1, hops):
-                hop_copy(g, hop).start()
-            pair_copy(g, 0).start()
+                peer = lax.rem(b + 2 * hop, nb)
+                strip_copy(g, b, hop_send.at[g], hop_recv.at[g], {"batch": peer}).start()
+            strip_copy(g, b, pair_send.at[g], pair_recv.at[g], {"batch": partner}).start()
+
+    def hop_all(g):
+        ref = wown.at[g, pl.ds(0, (hops - 1) * strip), :]
+        return remote(ref, ref, hop_send.at[g], hop_recv.at[g], {"batch": partner})
+
+    def pair_all(g):
+        ref = wown.at[g, pl.ds(0, hops * strip), :]
+        return remote(ref, ref, pair_send.at[g], pair_recv.at[g], {"batch": partner})
 
     def forward(g):
         @pl.when(z != g)
         def _():
+            hop_all(g).wait_recv()
             for hop in range(1, hops):
                 peer = lax.rem(b + 2 * hop, nb)
-                strip_copy(
-                    g, peer, hop_send.at[g, 0], hop_recv.at[g, peer], {"batch": peer}
-                ).wait_recv()
-                pair_copy(g, hop).start()
+                strip_copy(g, peer, pair_send.at[g], pair_recv.at[g], {"batch": partner}).start()
 
     def complete(g):
         @pl.when(z != g)
         def _():
-            for hop in range(hops):
-                who = 2 * hop + 1 - parity
-                strip_copy(
-                    g, who, pair_send.at[g, 0], pair_recv.at[g, who], {"batch": partner}
-                ).wait_recv()
+            pair_all(g).wait_recv()
 
     def flow_copy(f, k):
         to = jnp.where(f == 0, lax.rem(z + 1, n), lax.rem(z + n - 1, n))
         ref = flow.at[f, k]
-        return remote(ref, ref, flow_send.at[f, k], flow_recv.at[f, k], {"chan": to})
+        return remote(ref, ref, flow_send.at[f], flow_recv.at[f, k], {"chan": to})
 
     def chunk_of(f, position):
         q, r = lax.div(position, rows), lax.rem(position, rows)
@@ -219,34 +214,29 @@
 
         return carry
 
+    def near(q):
+        return jnp.where(z < mids, q, n - 1 - q)
+
+    def far(q):
+        return n - 1 - near(q)
+
     split = rows // 2
     lax.fori_loop(0, split, own_products, 0)
-    order = [g for q in range(mids) for g in (q, n - 1 - q)]
-    for g in order[:2]:
-        distribute(g)
+    distribute(near(0))
     lax.fori_loop(split, rows, own_products, 0)
-    for g in order[2:]:
-        distribute(g)
+    distribute(far(0))
+    for q in range(1, mids):
+        distribute(near(q))
+        distribute(far(q))
     act[:, 0] = jnp.zeros_like(act[:, 0])
     act[:, rows + 1] = jnp.zeros_like(act[:, 0])
     acc[...] = jnp.zeros_like(acc)
-    for g in order[:2]:
-        forward(g)
+    forward(near(0))
 
     def band_copy(slot, who, send, recv, device):
         ref = w2.at[:, :, band_of(who), slot_cols(slot)]
         return remote(ref, ref, send, recv, device)
 
-    def w2hop_copy(slot, hop):
-        peer = lax.rem(b + 2 * hop, nb)
-        return band_copy(slot, b, w2hop_send.at[slot, hop], w2hop_recv.at[slot, b], {"batch": peer})
-
-    def w2pair_copy(slot, hop):
-        who = lax.rem(b + 2 * hop, nb)
-        return band_copy(
-            slot, who, w2pair_send.at[slot, hop], w2pair_recv.at[slot, who], {"batch": partner}
-        )
-
     def each_slot(work):
         for slot in range(mids):
 
@@ -257,23 +247,32 @@
     def w2_distribute(slot):
         band_copy(slot, b, w2_send.at[0], w2_recv.at[slot], {"chan": z}).wait_recv()
         for hop in range(1, hops):
-            w2hop_copy(slot, hop).start()
-        w2pair_copy(slot, 0).start()
+            peer = lax.rem(b + 2 * hop, nb)
+            band_copy(slot, b, w2hop_send.at[slot], w2hop_recv.at[slot], {"batch": peer}).start()
+        band_copy(slot, b, w2pair_send.at[slot], w2pair_recv.at[slot], {"batch": partner}).start()
+
+    def w2hop_all(slot):
+        ref = w2.at[:, :, pl.ds(0, (hops - 1) * band), slot_cols(slot)]
+        return remote(ref, ref, w2hop_send.at[slot], w2hop_recv.at[slot], {"batch": partner})
+
+    def w2pair_all(slot):
+        ref = w2.at[:, :, pl.ds(0, hops * band), slot_cols(slot)]
+        return remote(ref, ref, w2pair_send.at[slot], w2pair_recv.at[slot], {"batch": partner})
 
     def w2_forward(slot):
+        w2hop_all(slot).wait_recv()
         for hop in range(1, hops):
             peer = lax.rem(b + 2 * hop, nb)
             band_copy(
-                slot, peer, w2hop_send.at[slot, 0], w2hop_recv.at[slot, peer], {"batch": peer}
-            ).wait_recv()
-            w2pair_copy(slot, hop).start()
+                slot, peer, w2pair_send.at[slot], w2pair_recv.at[slot], {"batch": partner}
+            ).start()
 
     def w2_complete(slot):
-        for hop in range(hops):
-            who = 2 * hop + 1 - parity
-            band_copy(
-                slot, who, w2pair_send.at[slot, 0], w2pair_recv.at[slot, who], {"batch": partner}
-            ).wait_recv()
+        w2pair_all(slot).wait_recv()
+
+    def gb_all():
+        ref = gb.at[pl.ds(0, n - 1)]
+        return remote(ref, ref, gb_send.at[0], gb_recv.at[0], {"chan": lax.rem(z + 1, n)})
 
     def end_group(q):
         return jnp.where(at_first, n - 1 - q, q)
@@ -302,19 +301,18 @@
         stat1[g, b, 1:2, :] = square1[g] - sum1[g] * extra
         stats_send(nb, b, stat1.at[g], st1_send.at[g], st1_recv.at[g])
 
-    def first_act(q):
+    def first_affine(q):
         g = end_group(q)
         stats_wait(nb, b, stat1.at[g], st1_send.at[g], st1_recv.at[g])
         mean, var = combine(stat1[g], local)
         scale = gb[g, 0:1, :] / jnp.sqrt(var + eps)
         bias = gb[g, 1:2, :]
 
-        def line(r, carry):
+        def line(r):
             value = (whole[lax.rem(q, 2), r] - mean) * scale + bias
             act[g, r + 1] = jnp.maximum(value, 0.0).astype(bf16)
-            return carry
-
-        lax.fori_loop(0, rows, line, 0)
+
+        return line
 
     def convolve(g, t):
         for col_tap in range(3):
@@ -335,39 +333,68 @@
 
     reach = SKEW * (n - 1) + SINK
 
+    pace = (rows + 1) // 2
+    packed = (n - 1) * (rows - pieces) + 1
+    lag1 = min(LAG, SKEW * mids)
+
+    def make(g, r):
+        @pl.when(jnp.logical_and(z != g, r < rows))
+        def _():
+            part[g * rows + r] = jnp.dot(img[r], wown[g], preferred_element_type=f32)
+
+    def produce(tick, pick):
+        @pl.when(jnp.logical_and(tick >= 0, tick < rows))
+        def _():
+            g = pick(0)
+
+            @pl.when(tick == 0)
+            def _():
+                complete(g)
+
+            make(g, tick)
+
+        late = tick - rows
+
+        @pl.when(jnp.logical_and(late >= 0, late < (mids - 1) * pace))
+        def _():
+            g, i = pick(1 + lax.div(late, pace)), lax.rem(late, pace)
+
+            @pl.when(i == 0)
+            def _():
+                complete(g)
+
+            make(g, 2 * i)
+            make(g, 2 * i + 1)
+
     def step(s, carry):
-        q, r = lax.div(s, rows), lax.rem(s, rows)
-
-        @pl.when(q < mids)
-        def _():
-            @pl.when(r == 0)
-            def _():
-                complete(q)
-                complete(n - 1 - q)
-
-            @pl.when(jnp.logical_and(r == rows // 2, q + 1 < mids))
-            def _():
-                forward(q + 1)
-                forward(n - 2 - q)
-
-            for g in (q, n - 1 - q):
-
-                @pl.when(z != g)
-                def _():
-                    part[g * rows + r] = jnp.dot(img[r], wown[g], preferred_element_type=f32)
+        @pl.when(s == 2)
+        def _():
+            forward(far(0))
+
+        for q in range(1, mids):
+
+            @pl.when(s == 6 + (q - 1) * pace)
+            def _():
+                forward(near(q))
+                forward(far(q))
+
+        produce(s, near)
+        produce(s - lag1, far)
+
+        for extra in range(2):
+            position = rows + 2 * (s - rows) + extra
+            k = chunk_of(side, position)
+
+            @pl.when(jnp.logical_and(at_end, jnp.logical_and(s >= rows, position < chunks)))
+            def _():
+                flow[side, k] = part[k].astype(bf16)
+                flow_copy(side, k).start()
 
         for f in range(2):
-            from_start = z if f == 0 else n - 1 - z
-            position = s - SKEW * from_start
+            position = s - SKEW * (z if f == 0 else n - 1 - z)
             k = chunk_of(f, position)
-            inside = jnp.logical_and(position >= 0, position < chunks)
-
-            @pl.when(jnp.logical_and(inside, jnp.logical_and(from_start == 0, position >= rows)))
-            def _():
-                flow[f, k] = part[k].astype(bf16)
-                flow_copy(f, k).start()
-
-            @pl.when(jnp.logical_and(inside, inner))
+
+            @pl.when(jnp.logical_and(inner, jnp.logical_and(position >= 0, position < chunks)))
             def _():
                 flow_copy(f, k).wait_recv()
                 flow[f, k] = (part[k] + flow[f, k].astype(f32)).astype(bf16)
@@ -375,49 +402,53 @@
 
         @pl.when(at_end)
         def _():
-            @pl.when(s == rows // 2)
+            position = s - reach
+            after = position - (rows - 1)
+
+            @pl.when(position == 0)
             def _():
                 each_slot(w2_distribute)
 
-            @pl.when(s == rows + rows // 2)
+            @pl.when(after == packed - 6)
             def _():
                 each_slot(w2_forward)
 
-            position = s - reach
+            @pl.when(after == packed)
+            def _():
+                w2_load.wait()
+                each_slot(w2_complete)
 
             @pl.when(position >= 0)
             def _():
                 finalize(position)
 
-            after = position - (rows - 1)
-
             @pl.when(after >= 0)
             def _():
                 q, v = lax.div(after, rows), lax.rem(after, rows)
-                g = end_group(q)
 
                 @pl.when(v == 0)
                 def _():
-                    first_stats(g)
+                    first_stats(end_group(q))
 
                 @pl.when(v == 4)
                 def _():
                     @pl.when(q == 0)
                     def _():
-                        for to in range(n):
-
-                            @pl.when(z != to)
-                            def _():
-                                gb_copy(to, to).wait_recv()
-
-                        w2_load.wait()
-                        each_slot(w2_complete)
-
-                    first_act(q)
-
-                @pl.when(jnp.logical_and(v >= 5, v < 5 + pieces))
-                def _():
-                    convolve(g, v - 5)
+                        gb_all().wait_recv()
+
+                    line = first_affine(q)
+
+                    def each_line(r, carry):
+                        line(r)
+                        return carry
+
+                    lax.fori_loop(0, rows, each_line, 0)
+
+            item = after - packed
+
+            @pl.when(item >= 0)
+            def _():
+                convolve(end_group(lax.div(item, pieces)), lax.rem(item, pieces))
 
         return carry
 
@@ -427,7 +458,7 @@
         to = jnp.where(f == 0, lax.rem(z + 1, n), lax.rem(z + n - 1, n))
         line, part_of = lax.div(u, 2), lax.rem(u, 2)
         ref = sec.at[f, line, :, pl.ds(pl.multiple_of(part_of * unit, 128), unit)]
-        return remote(ref, ref, sec_send.at[f, u], sec_recv.at[f, u], {"chan": to})
+        return remote(ref, ref, sec_send.at[f], sec_recv.at[f, u], {"chan": to})
 
     def sec_start(u, carry):
         sec_copy(side, u).start()
@@ -439,11 +470,18 @@
     @pl.when(at_end)
     def _():
         last = end_group(n - 1)
-        first_act(n - 1)
+        line = first_affine(n - 1)
+        line(0)
         sum2[...] = jnp.zeros_like(sum2)
         square2[...] = jnp.zeros_like(square2)
 
         def tail(t, carry):
+            for ahead in range(1, join + 1):
+
+                @pl.when(t * join + ahead < rows)
+                def _():
+                    line(t * join + ahead)
+
             convolve(last, t)
             lines = pl.ds(t * join, join)
             total = acc[lines].reshape(tall, half)
@@ -467,8 +505,8 @@
         extra = sum2[...] / local
         stat2[b, 0:1, :] = shift2[...] + extra
         stat2[b, 1:2, :] = square2[...] - sum2[...] * extra
-        stats_send(nb, b, stat2, st2_send, st2_recv)
-        stats_wait(nb, b, stat2, st2_send, st2_recv)
+        stats_send(nb, b, stat2, st2_send.at[0], st2_recv.at[0])
+        stats_wait(nb, b, stat2, st2_send.at[0], st2_recv.at[0])
         mean, var = combine(stat2[...], local)
         inverse = 1.0 / jnp.sqrt(var + eps)
         for i in range(mids):
@@ -550,22 +588,17 @@
     extra = sum3[...] / local
     stat3[b, 0:1, :] = shift3[...] + extra
     stat3[b, 1:2, :] = square3[...] - sum3[...] * extra
-    stats_send(nb, b, stat3, st3_send, st3_recv)
-
+    stats_send(nb, b, stat3, st3_send.at[0], st3_recv.at[0])
+
+    sent = wown.at[0, pl.ds(0, (n - 1) * strip), :]
+    remote(sent, sent, w1_send.at[0], w1_recv.at[0], {"batch": partner}).wait_send()
+    gb_all().wait_send()
     for to in range(n):
 
         @pl.when(z != to)
         def _():
-            w1_copy(to).wait_send()
-            gb_copy(to, z).wait_send()
-            for hop in range(1, hops):
-                hop_copy(to, hop).wait_send()
-            for hop in range(hops):
-                pair_copy(to, hop).wait_send()
-
-            @pl.when(inner)
-            def _():
-                gb_copy(to, to).wait_recv()
+            hop_all(to).wait_send()
+            pair_all(to).wait_send()
 
             @pl.when(at_end)
             def _():
@@ -573,13 +606,12 @@
 
     @pl.when(inner)
     def _():
+        gb_all().wait_recv()
         w2_copy.wait_send()
 
     def w2_drain(slot):
-        for hop in range(1, hops):
-            w2hop_copy(slot, hop).wait_send()
-        for hop in range(hops):
-            w2pair_copy(slot, hop).wait_send()
+        w2hop_all(slot).wait_send()
+        w2pair_all(slot).wait_send()
 
     @pl.when(at_end)
     def _():
@@ -589,39 +621,22 @@
 
         @pl.when(z != (n - 1) * (1 - f))
         def _():
-            def drain_flow(k, carry):
-                flow_copy(f, k).wait_send()
-                return carry
-
-            def drain_sec(u, carry):
-                sec_copy(f, u).wait_send()
-                return carry
-
-            lax.fori_loop(0, chunks, drain_flow, 0)
-            lax.fori_loop(0, units, drain_sec, 0)
-
-    stats_wait(nb, b, stat3, st3_send, st3_recv)
+            right = {"chan": lax.rem(z + 1, n)}
+            remote(flow.at[f], flow.at[f], flow_send.at[f], flow_recv.at[f, 0], right).wait_send()
+            remote(sec.at[f], sec.at[f], sec_send.at[f], sec_recv.at[f, 0], right).wait_send()
+
+    stats_wait(nb, b, stat3, st3_send.at[0], st3_recv.at[0])
     mean3, var3 = combine(stat3[...], local)
     scale3 = gain3[...] / jnp.sqrt(var3 + eps)
     bias3_value = bias3[...]
-
-    def out_copy(t):
-        return pltpu.make_async_copy(outv.at[t], out_hbm.at[t], out_sem.at[t])
 
     def finish(t, carry):
         kept = img[pl.ds(t * join, join)].reshape(tall, out_local).astype(f32)
         value = (third[t] - mean3) * scale3 + bias3_value + kept
         outv[t] = jnp.maximum(value, 0.0).astype(bf16)
-        out_copy(t).start()
         return carry
 
     lax.fori_loop(0, pieces, finish, 0)
-
-    def out_drain(t, carry):
-        out_copy(t).wait()
-        return carry
-
-    lax.fori_loop(0, pieces, out_drain, 0)
 
 
 def body(
@@ -654,9 +669,9 @@
     flat = images.transpose(1, 2, 0, 3).reshape(rows, height, depth)
     out = pl.pallas_call(
         functools.partial(block_kernel, n, nb, imgs),
-        out_shape=jax.ShapeDtypeStruct((pieces, tall, out_local), bf16),
+        out_shape=pltpu.VMEM((pieces, tall, out_local), bf16),
         in_specs=[anywhere, anywhere, vmem, vmem, anywhere, vmem, vmem, anywhere, vmem, vmem],
-        out_specs=anywhere,
+        out_specs=vmem,
         scratch_shapes=[
             pltpu.VMEM((rows, height, depth), bf16),
             pltpu.VMEM(reduce_weight.shape, bf16),
@@ -682,18 +697,19 @@
             pltpu.VMEM((pieces, tall, out_local), f32),
         ]
         + [pltpu.VMEM((1, out_local), f32)] * 3
-        + [pltpu.VMEM((nb, 2, out_local), f32), pltpu.VMEM((pieces, tall, out_local), bf16)]
-        + [dma((4,)), dma((pieces,))]
+        + [pltpu.VMEM((nb, 2, out_local), f32)]
+        + [dma((4,))]
+        + [dma((1,))] * 2
+        + [dma((1,)), dma((n,))]
         + [dma((n,))] * 4
-        + [dma((n, nb // 2)), dma((n, nb))] * 2
-        + [dma((2, chunks))] * 2
-        + [dma((n, nb))] * 2
+        + [dma((2,)), dma((2, chunks))]
+        + [dma((n,))] * 2
         + [dma((1,)), dma((mids,))]
-        + [dma((mids, nb // 2)), dma((mids, nb))] * 2
-        + [dma((2, 2 * rows))] * 2
-        + [dma((nb,))] * 2
+        + [dma((mids,))] * 4
+        + [dma((2,)), dma((2, 2 * rows))]
+        + [dma((1,))] * 2
         + [dma((n,)), dma((2,))]
-        + [dma((nb,))] * 2,
+        + [dma((1,))] * 2,
         compiler_params=pltpu.CompilerParams(
             collective_id=0, has_side_effects=True, vmem_limit_bytes=LIMIT
         ),

time: 166 us -> 151 us (0.910)
  Pallas kernels: 162 us -> 149 us
  local copies, waits for them, and re-layouts: 3.96 us -> 1.69 us
    pallas_call x1, Pallas kernels: 162 us -> 149 us  [body(): pl.pallas_call(functools.partial(block_kernel, n, nb, imgs), out_shape=pl...]
    unnamed x1, local copies, waits for them, and re-layouts: 3.96 us -> 1.69 us
where the time goes in v2:
time: 151 us
  Pallas kernels  149 us (99%)
  local copies, waits for them, and re-layouts  1.69 us (1%)
    pallas_call x1, Pallas kernels, body(): pl.pallas_call(functools.partial(block_kernel, n, nb, imgs), out_shape=pl...  149 us

profile of v2, /device:TPU:0, one launch (start us, length us, event | category | flops | bytes accessed | tf_op | source)
XLA Modules:
  0.0 150.6 jit_solution(897190437053609578)
XLA Ops:
  0.0 148.9 %block.1 = bf16[7,224,1024]{2,1,0:T(8,128)(2,1)S(1)} custom-call(bf16[14,112,1024]{2,1,0:T(8,128)(2,1)} %bitcast.13, bf16[4096,256]{1,0:T(8,128)(2,1)} %w1_hbm.1, f32[1,256]{1,0:T(1,128)} %bitcast.16, f32[1,256]{1,0:T(1,128)} %bitcast.17, bf16[3,3,1024,256]{3,2,1,0:T(8,128)(2,1)} %sw_hbm.1, f32[1,256]{1,0:T(1,128)} %bitcast.18, f32[1,256]{1,0:T(1,128)} %bitcast.19, ...), custom_call_target="tpu_custom_call" | custom-call | tf_op jit(solution)/shard_map/block/pallas_call | solution.py:670
  148.9 1.7 %copy.12 = bf16[8,14,14,1024]{3,0,2,1:T(8,128)(2,1)} copy(bf16[8,14,14,1024]{3,0,2,1:T(8,128)(2,1)S(1)} %bitcast.12) | data formatting | bytes 6422528

commit v3 on v2

v3 whole, which is shorter than its diff:
```python
import functools

import jax
import jax.numpy as jnp
from jax import lax
from jax.experimental import pallas as pl
from jax.experimental.pallas import tpu as pltpu
from jax.sharding import PartitionSpec as P

eps = 0.001
MESH = pl.DeviceIdType.MESH
LIMIT = 59 * 1024 * 1024
SKEW = 3
EXTRA = 1
HELD = 4
SETTLE = 8
OUTER_GIVE = (0, 3, 6)
INNER_SHARE = (0, 18, 22)
OUTER_SHARE = (0, 2, 4)
INNER_MORE = (1, 26, 33)
OUTER_MORE = (21, 25, 33)
MORE_CHAIN = (1, 3, 5)


def remote(src, dst, send, recv, device):
    return pltpu.make_async_remote_copy(
        src_ref=src, dst_ref=dst, send_sem=send, recv_sem=recv,
        device_id=device, device_id_type=MESH,
    )


def greet(n, nb, z, b):
    barrier = pltpu.get_barrier_semaphore()
    for off in range(1, n):
        pl.semaphore_signal(
            barrier, inc=1, device_id={"chan": lax.rem(z + off, n)}, device_id_type=MESH
        )
    for off in range(1, nb):
        pl.semaphore_signal(
            barrier, inc=1, device_id={"batch": lax.rem(b + off, nb)}, device_id_type=MESH
        )
    pl.semaphore_wait(barrier, n + nb - 2)


def stats_send(nb, b, stats, send, recv):
    for off in range(1, nb):
        peer = lax.rem(b + off, nb)
        remote(stats.at[b], stats.at[b], send, recv, {"batch": peer}).start()


def stats_wait(nb, b, stats, send, recv):
    others = stats.at[pl.ds(0, nb - 1)]
    remote(others, others, send, recv, {"batch": lax.rem(b + 1, nb)}).wait()


def combine(stats, local):
    nb = stats.shape[0]
    means = stats[..., 0:1, :]
    mean = jnp.sum(means, axis=0) / nb
    away = means - mean[None]
    spread = jnp.sum(stats[..., 1:2, :], axis=0) + local * jnp.sum(away * away, axis=0)
    return mean, spread / (local * nb)


def column_sum(value):
    return jnp.sum(value, axis=0, keepdims=True)


def block_kernel(
    n, nb, imgs,
    img_hbm, w1_hbm, gain1, bias1, sw_hbm, gain2, bias2, w3_hbm, gain3, bias3,
    outv,
    img, w1, wown, part, whole, flow, gb, shift1, sum1, square1, stat1, act, w2, acc, sec,
    shift2, sum2, square2, stat_out, stat_keep, affine, w3, third, shift3, sum3, square3, stat3,
    load_sem,
    gb_send, gb_recv, w1_send, w1_recv, hop_send, hop_recv, pair_send, pair_recv,
    flow_send, flow_recv, st1_send, st1_recv,
    w2_send, w2_recv, w2hop_send, w2hop_recv, w2pair_send, w2pair_recv,
    sec_send, sec_recv, st2_send, st2_recv, st4_send, st4_recv, aff_send, aff_recv, st3_send, st3_recv,
):
    z, b = lax.axis_index("chan"), lax.axis_index("batch")
    rows, height, depth = img.shape
    width = wown.shape[2]
    slots = w2.shape[0]
    pieces, tall, out_local = third.shape
    join = rows // pieces
    mids = n // 2
    more = slots - mids
    lacking = mids - more
    hops = nb // 2
    chunks = n * rows
    strip = depth // nb
    band = n * width // nb
    local = rows * height
    per_piece = lacking * join
    units = lacking * rows
    partner = b + 1 - 2 * lax.rem(b, 2)
    at_first, at_last = z == 0, z == n - 1
    at_end = jnp.logical_or(at_first, at_last)
    inner = jnp.logical_not(at_end)
    side = jnp.where(z < mids, 0, 1)
    gone = jnp.where(z < mids, mids - 1 - z, z - mids)
    first_block = side * (mids - more)
    my_slot = z - first_block
    half_slot = side * more
    more_slot = (1 - side) * mids
    out_slot = side * (slots - lacking)
    keep_slot = (1 - side) * lacking
    late_flow = 1 - side
    late_skew = SKEW * jnp.maximum(z, n - 1 - z)
    early_skew = SKEW * jnp.minimum(z, n - 1 - z)
    f32, bf16 = jnp.float32, jnp.bfloat16

    w1_load = pltpu.make_async_copy(w1_hbm, w1, load_sem.at[0])
    w1_load.start()
    img_load = pltpu.make_async_copy(img_hbm, img, load_sem.at[1])
    img_load.start()
    w3_load = pltpu.make_async_copy(w3_hbm, w3, load_sem.at[2])
    w3_load.start()

    w2_load = pltpu.make_async_copy(sw_hbm, w2.at[my_slot], load_sem.at[3])
    w2_load.start()
    gb[z, 0:1, :] = gain1[...]
    gb[z, 1:2, :] = bias1[...]
    gb[z, 2:3, :] = gain2[...]
    gb[z, 3:4, :] = bias2[...]
    greet(n, nb, z, b)

    def rows_of(who):
        return pl.ds(pl.multiple_of(who * strip, 16), strip)

    def w1_copy(to):
        src = w1.at[pl.ds(pl.multiple_of(to * depth + b * strip, 16), strip), :]
        return remote(src, wown.at[z, rows_of(b), :], w1_send.at[0], w1_recv.at[z], {"chan": to})

    def gb_copy(to, slot):
        return remote(gb.at[z], gb.at[slot], gb_send.at[0], gb_recv.at[0], {"chan": to})

    def band_of(who):
        return pl.ds(pl.multiple_of(who * band, 16), band)

    w1_load.wait()
    for far in range(n - 1, 0, -1):

        @pl.when(z + far < n)
        def _():
            w1_copy(z + far).start()

        @pl.when(z - far >= 0)
        def _():
            w1_copy(z - far).start()

    for off in range(1, n):
        gb_copy(lax.rem(z + off, n), z).start()

    def band_ref(slot, row_tap, who):
        return w2.at[slot, row_tap, :, band_of(who), :]

    def w2_give(row_tap, to, slot, kind):
        src = sw_hbm.at[row_tap, :, band_of(b), :]
        return remote(
            src, band_ref(slot, row_tap, b), w2_send.at[kind], w2_recv.at[slot, row_tap],
            {"chan": to},
        )

    def half_give(row_tap):
        for off in range(1, mids):
            to = side * mids + lax.rem(z - side * mids + off, mids)
            w2_give(row_tap, to, my_slot, 0).start()

    for row_tap in range(3):
        if more:

            @pl.when(gone == 0)
            def _():
                to = jnp.where(side == 0, mids, mids - 1)
                w2_give(row_tap, to, jnp.where(side == 0, 0, mids), 1).start()

        if row_tap == 0:
            half_give(row_tap)
        else:

            @pl.when(inner)
            def _():
                half_give(row_tap)

    def strip_copy(g, who, send, recv, device):
        ref = wown.at[g, rows_of(who), :]
        return remote(ref, ref, send, recv, device)

    def distribute(g):
        @pl.when(z != g)
        def _():
            strip_copy(g, b, w1_send.at[0], w1_recv.at[g], {"chan": g}).wait_recv()
            for hop in range(1, hops):
                peer = lax.rem(b + 2 * hop, nb)
                strip_copy(g, b, hop_send.at[g], hop_recv.at[g], {"batch": peer}).start()
            strip_copy(g, b, pair_send.at[g], pair_recv.at[g], {"batch": partner}).start()

    def hop_all(g):
        ref = wown.at[g, pl.ds(0, (hops - 1) * strip), :]
        return remote(ref, ref, hop_send.at[g], hop_recv.at[g], {"batch": partner})

    def pair_all(g):
        ref = wown.at[g, pl.ds(0, hops * strip), :]
        return remote(ref, ref, pair_send.at[g], pair_recv.at[g], {"batch": partner})

    def forward(g):
        @pl.when(z != g)
        def _():
            hop_all(g).wait_recv()
            for hop in range(1, hops):
                peer = lax.rem(b + 2 * hop, nb)
                strip_copy(g, peer, pair_send.at[g], pair_recv.at[g], {"batch": partner}).start()

    def complete(g):
        @pl.when(z != g)
        def _():
            pair_all(g).wait_recv()

    def flow_copy(f, k):
        to = jnp.where(f == 0, lax.rem(z + 1, n), lax.rem(z + n - 1, n))
        ref = flow.at[f, k]
        return remote(ref, ref, flow_send.at[f], flow_recv.at[f, k], {"chan": to})

    img_load.wait()

    def own_products(r, carry):
        k = z * rows + r
        value = jnp.dot(
            img[r], w1[pl.ds(pl.multiple_of(z * depth, 16), depth), :], preferred_element_type=f32
        )
        part[k] = value

        @pl.when(at_first)
        def _():
            flow[0, k] = value.astype(bf16)
            flow_copy(0, k).start()

        return carry

    lax.fori_loop(0, rows, own_products, 0)
    for g in range(n):
        distribute(g)
    act[:, 0] = jnp.zeros_like(act[:, 0])
    act[:, rows + 1] = jnp.zeros_like(act[:, 0])

    def clear(r, carry):
        acc[:, r] = jnp.zeros_like(acc[:, r])
        return carry

    lax.fori_loop(0, rows, clear, 0)
    forward(0)

    def w2_share(slot, row_tap):
        ref = band_ref(slot, row_tap, b)
        for hop in range(1, hops):
            peer = lax.rem(b + 2 * hop, nb)
            remote(ref, ref, w2hop_send.at[slot], w2hop_recv.at[slot], {"batch": peer}).start()
        remote(ref, ref, w2pair_send.at[slot], w2pair_recv.at[slot], {"batch": partner}).start()

    def w2_arrive(slot, row_tap):
        ref = band_ref(slot, row_tap, b)
        remote(ref, ref, w2_send.at[0], w2_recv.at[slot, row_tap], {"chan": z}).wait_recv()

    def half_share(row_tap):
        def work(slot):
            w2_arrive(slot, row_tap)
            w2_share(slot, row_tap)

        half_slots(work)

    def w2_chain(row_tap):
        ref = band_ref(more_slot, row_tap, b)
        to = jnp.where(side == 0, lax.rem(z + n - 1, n), lax.rem(z + 1, n))
        return remote(ref, ref, w2_send.at[2], w2_recv.at[more_slot, row_tap], {"chan": to})

    def w2hop_all(slot):
        ref = w2.at[slot, :, :, pl.ds(0, (hops - 1) * band), :]
        return remote(ref, ref, w2hop_send.at[slot], w2hop_recv.at[slot], {"batch": partner})

    def w2pair_all(slot):
        ref = w2.at[slot, :, :, pl.ds(0, hops * band), :]
        return remote(ref, ref, w2pair_send.at[slot], w2pair_recv.at[slot], {"batch": partner})

    def w2_forward(slot):
        w2hop_all(slot).wait_recv()
        for row_tap in range(3):
            for hop in range(1, hops):
                ref = band_ref(slot, row_tap, lax.rem(b + 2 * hop, nb))
                remote(
                    ref, ref, w2pair_send.at[slot], w2pair_recv.at[slot], {"batch": partner}
                ).start()

    def half_slots(work):
        for off in range(1, mids):
            work(half_slot + lax.rem(my_slot - half_slot + off, mids))

    def gb_all():
        ref = gb.at[pl.ds(0, n - 1)]
        return remote(ref, ref, gb_send.at[0], gb_recv.at[0], {"chan": lax.rem(z + 1, n)})

    def finalize(k, value):
        g, r = lax.div(k, rows), lax.rem(k, rows)
        whole[lax.rem(g, 2), r] = value

        @pl.when(r == 0)
        def _():
            shift1[g] = column_sum(value) / height
            sum1[g] = jnp.zeros_like(sum1[g])
            square1[g] = jnp.zeros_like(square1[g])

        moved = value - shift1[g]
        sum1[g] += column_sum(moved)
        square1[g] += column_sum(moved * moved)

    def first_stats(g):
        extra = sum1[g] / local
        stat1[g, b, 0:1, :] = shift1[g] + extra
        stat1[g, b, 1:2, :] = square1[g] - sum1[g] * extra
        stats_send(nb, b, stat1.at[g], st1_send.at[g], st1_recv.at[g])

    def first_affine(g):
        stats_wait(nb, b, stat1.at[g], st1_send.at[g], st1_recv.at[g])
        mean, var = combine(stat1[g], local)
        scale = gb[g, 0:1, :] / jnp.sqrt(var + eps)
        bias = gb[g, 1:2, :]

        def line(r):
            value = (whole[lax.rem(g, 2), r] - mean) * scale + bias
            act[g, r + 1] = jnp.maximum(value, 0.0).astype(bf16)

        return line

    def convolve(g, t, slot):
        lines = pl.ds(t * join, join)
        for col_tap in range(3):
            total = None
            for row_tap in range(3):
                window = act[g, pl.ds(t * join + row_tap, join)].reshape(tall, width)
                weight = w2[slot, row_tap, col_tap, pl.ds(pl.multiple_of(g * width, 128), width), :]
                term = jnp.dot(window, weight, preferred_element_type=f32)
                total = term if total is None else total + term
            total = total.reshape(join, height, width)
            if col_tap == 0:
                acc[slot, lines, imgs:, :] += total[:, : height - imgs]
            elif col_tap == 1:
                acc[slot, lines] += total
            else:
                acc[slot, lines, : height - imgs, :] += total[:, imgs:]

    last = n - 1
    all_begin = last * rows - pieces + 1
    more_begin = all_begin - pieces
    half_begin = more_begin - (last - 1) * pieces

    def step(s, carry):
        for g in range(1, n):

            @pl.when(s == (g - 1) * (rows // 2) + 2)
            def _():
                forward(g)

        for row_tap in range(3):
            if row_tap:

                @pl.when(jnp.logical_and(at_end, s == OUTER_GIVE[row_tap]))
                def _():
                    half_give(row_tap)

            if more:

                @pl.when(s == jnp.where(at_end, OUTER_MORE[row_tap], MORE_CHAIN[row_tap]))
                def _():
                    w2_arrive(more_slot, row_tap)

                    @pl.when(inner)
                    def _():
                        w2_chain(row_tap).start()

                @pl.when(s == jnp.where(at_end, OUTER_MORE[row_tap], INNER_MORE[row_tap]))
                def _():
                    w2_share(more_slot, row_tap)

            @pl.when(s == jnp.where(at_end, OUTER_SHARE[row_tap], INNER_SHARE[row_tap]))
            def _():
                half_share(row_tap)

        for extra in range(2):
            k = 2 * s + extra
            g, r = lax.div(k, rows), lax.rem(k, rows)

            @pl.when(k < chunks)
            def _():
                @pl.when(r == 0)
                def _():
                    complete(g)

                @pl.when(z != g)
                def _():
                    part[k] = jnp.dot(img[r], wown[g], preferred_element_type=f32)

                @pl.when(jnp.logical_and(at_end, jnp.logical_or(at_last, k >= rows)))
                def _():
                    flow[side, k] = part[k].astype(bf16)
                    flow_copy(side, k).start()

        early = s - early_skew

        @pl.when(jnp.logical_and(inner, jnp.logical_and(early >= 0, early < chunks)))
        def _():
            flow_copy(side, early).wait_recv()
            flow[side, early] = (part[early] + flow[side, early].astype(f32)).astype(bf16)
            flow_copy(side, early).start()

        late = s - late_skew
        after = late - (rows - 1)

        @pl.when(late >= 0)
        def _():
            flow_copy(late_flow, late).wait_recv()
            coming = flow[late_flow, late].astype(f32)

            @pl.when(inner)
            def _():
                flow[late_flow, late] = (part[late] + coming).astype(bf16)
                flow_copy(late_flow, late).start()
                finalize(late, flow[side, late].astype(f32) + coming)

            @pl.when(at_end)
            def _():
                finalize(late, part[late] + coming)

        @pl.when(after == half_begin - 6)
        def _():
            half_slots(w2_forward)

        @pl.when(after == half_begin - 1)
        def _():
            w2_load.wait()
            half_slots(lambda slot: w2pair_all(slot).wait_recv())

        if more:

            @pl.when(after == more_begin - 5)
            def _():
                w2_forward(more_slot)

            @pl.when(after == more_begin - 1)
            def _():
                w2pair_all(more_slot).wait_recv()

        @pl.when(after >= 0)
        def _():
            g, v = lax.div(after, rows), lax.rem(after, rows)

            @pl.when(v == 0)
            def _():
                first_stats(g)

            @pl.when(v == SETTLE)
            def _():
                @pl.when(g == 0)
                def _():
                    gb_all().wait_recv()

                line = first_affine(g)

                def each_line(r, carry):
                    line(r)
                    return carry

                lax.fori_loop(0, rows, each_line, 0)

        item = after - half_begin

        @pl.when(jnp.logical_and(item >= 0, item < (last - 1) * pieces))
        def _():
            for i in range(mids):
                convolve(lax.div(item, pieces), lax.rem(item, pieces), half_slot + i)

        if more:

            @pl.when(jnp.logical_and(after >= more_begin, after < more_begin + pieces))
            def _():
                for g in range(last - 1):
                    convolve(g, after - more_begin, more_slot)

        @pl.when(after >= all_begin)
        def _():
            for slot in range(slots):
                convolve(last - 1, after - all_begin, slot)

        return carry

    lax.fori_loop(0, chunks + late_skew, step, 0)

    def sec_copy(f, u):
        to = jnp.where(f == 0, lax.rem(z + 1, n), lax.rem(z + n - 1, n))
        t, rest = lax.div(u, per_piece), lax.rem(u, per_piece)
        block = lax.div(rest, join) + f * (mids + more)
        ref = sec.at[block, t * join + lax.rem(rest, join)]
        kind = jnp.where(f == side, 0, 1)
        return remote(ref, ref, sec_send.at[kind], sec_recv.at[u], {"chan": to})

    def sec_start(u, carry):
        sec_copy(side, u).start()
        return carry

    far_block = (1 - side) * (mids + more)
    near_block = side * (mids + more)

    def affine_copy(to, block):
        ref = affine.at[pl.ds(block, lacking)]
        return remote(ref, ref, aff_send.at[to], aff_recv.at[0], {"chan": to})

    def relay(tick):
        u = tick - SKEW * gone

        @pl.when(jnp.logical_and(u >= 0, u < units))
        def _():
            sec_copy(1 - side, u).wait_recv()

            @pl.when(inner)
            def _():
                sec_copy(1 - side, u).start()

    line = first_affine(last)
    line(0)
    sum2[...] = jnp.zeros_like(sum2)
    square2[...] = jnp.zeros_like(square2)

    def measure(t, slot):
        convolve(last, t, slot)
        lines = pl.ds(t * join, join)
        total = acc[slot, lines].reshape(tall, width)

        @pl.when(t == 0)
        def _():
            shift2[slot] = column_sum(total) / tall

        moved = total - shift2[slot]
        sum2[slot] += column_sum(moved)
        square2[slot] += column_sum(moved * moved)
        sec[first_block + slot, lines] = moved.astype(bf16).reshape(join, height, width)

    def record(stats, i, slot):
        extra = sum2[slot] / local
        stats[b, i, 0:1, :] = shift2[slot] + extra
        stats[b, i, 1:2, :] = square2[slot] - sum2[slot] * extra

    def derive(stats, base, count):
        mean, var = combine(stats[...], local)
        inverse = 1.0 / jnp.sqrt(var + eps)
        for i in range(count):
            block = first_block + base + i
            scale = gb[block, 2:3, :] * inverse[i]
            affine[block, 0:1, :] = scale
            affine[block, 1:2, :] = (shift2[base + i] - mean[i]) * scale + gb[block, 3:4, :]

    def outgoing(t, carry):
        for ahead in range(1, join + 1):

            @pl.when(t * join + ahead < rows)
            def _():
                line(t * join + ahead)

        for i in range(lacking):
            measure(t, out_slot + i)

        @pl.when(jnp.logical_and(gone == 0, t < HELD))
        def _():
            lax.fori_loop(t * per_piece, (t + 1) * per_piece, sec_start, 0)

        return carry

    lax.fori_loop(0, pieces, outgoing, 0)
    for i in range(lacking):
        record(stat_out, i, out_slot + i)
    stats_send(nb, b, stat_out, st2_send.at[0], st2_recv.at[0])

    def keeping(t, carry):
        for i in range(2 * more):
            measure(t, keep_slot + i)

        relay(t)
        return carry

    begun = pieces // 2 if more else 0
    if more:
        lax.fori_loop(0, begun, keeping, 0)
    stats_wait(nb, b, stat_out, st2_send.at[0], st2_recv.at[0])
    derive(stat_out, out_slot, lacking)

    @pl.when(gone == 0)
    def _():
        for i in range(mids):
            affine_copy((1 - side) * mids + i, near_block).start()
        lax.fori_loop(min(HELD, pieces) * per_piece, units, sec_start, 0)

    if more:
        lax.fori_loop(begun, pieces, keeping, 0)
        for i in range(2 * more):
            record(stat_keep, i, keep_slot + i)
        stats_send(nb, b, stat_keep, st4_send.at[0], st4_recv.at[0])
        for tick in range(pieces, pieces + 2):
            relay(tick)
        stats_wait(nb, b, stat_keep, st4_send.at[0], st4_recv.at[0])
        derive(stat_keep, keep_slot, 2 * more)

    w3_load.wait()
    sum3[...] = jnp.zeros_like(sum3)
    square3[...] = jnp.zeros_like(square3)
    lag = SKEW * gone

    def expand(t):
        values = []
        for block in range(n):
            value = sec[block, pl.ds(t * join, join)].reshape(tall, width).astype(f32)
            value = value * affine[block, 0:1, :] + affine[block, 1:2, :]
            values.append(jnp.maximum(value, 0.0).astype(bf16))
        total = jnp.dot(
            jnp.concatenate(values, axis=1), w3[...], preferred_element_type=f32
        )
        third[t] = total

        @pl.when(t == 0)
        def _():
            shift3[...] = column_sum(total) / tall

        moved = third[t] - shift3[...]
        sum3[...] += column_sum(moved)
        square3[...] += column_sum(moved * moved)

    relay_first = pieces + 2 if more else 0
    ready = relay_first + 1

    def relay_step(s, carry):
        relay(s)

        @pl.when(s == ready)
        def _():
            remote(
                affine.at[pl.ds(far_block, lacking)], affine.at[pl.ds(far_block, lacking)],
                aff_send.at[0], aff_recv.at[0], {"chan": lax.rem(z + 1, n)},
            ).wait_recv()

        t_late = s - ready
        catching = jnp.logical_and(t_late >= 0, t_late < pieces)
        catching = jnp.logical_and(catching, per_piece * (t_late + 1) - 1 + lag <= s)
        fresh = s - (per_piece - 1) - lag
        t_fresh = lax.div(fresh, per_piece)
        arriving = jnp.logical_and(fresh >= 0, lax.rem(fresh, per_piece) == 0)
        arriving = jnp.logical_and(arriving, t_fresh < pieces)
        arriving = jnp.logical_and(arriving, ready + t_fresh < s)

        @pl.when(jnp.logical_or(catching, arriving))
        def _():
            expand(jnp.where(catching, t_late, t_fresh))

        return carry

    relay_last = jnp.maximum(units + lag, ready + pieces)
    lax.fori_loop(relay_first, relay_last, relay_step, 0)

    extra = sum3[...] / local
    stat3[b, 0:1, :] = shift3[...] + extra
    stat3[b, 1:2, :] = square3[...] - sum3[...] * extra
    stats_send(nb, b, stat3, st3_send.at[0], st3_recv.at[0])

    sent = wown.at[0, pl.ds(0, (n - 1) * strip), :]
    remote(sent, sent, w1_send.at[0], w1_recv.at[0], {"batch": partner}).wait_send()
    gb_all().wait_send()
    for to in range(n):

        @pl.when(z != to)
        def _():
            hop_all(to).wait_send()
            pair_all(to).wait_send()

    w2_sent = w2.at[0, :, :, pl.ds(0, (mids - 1) * band), :]
    right = {"chan": lax.rem(z + 1, n)}
    remote(w2_sent, w2_sent, w2_send.at[0], w2_recv.at[0, 0], right).wait_send()
    half_slots(lambda slot: w2hop_all(slot).wait_send())
    half_slots(lambda slot: w2pair_all(slot).wait_send())
    if more:
        w2_one = w2.at[0, :, :, pl.ds(0, band), :]
        w2hop_all(more_slot).wait_send()
        w2pair_all(more_slot).wait_send()

        @pl.when(inner)
        def _():
            remote(w2_one, w2_one, w2_send.at[2], w2_recv.at[0, 0], right).wait_send()

        @pl.when(gone == 0)
        def _():
            remote(w2_one, w2_one, w2_send.at[1], w2_recv.at[0, 0], right).wait_send()

    for f in range(2):

        @pl.when(z != (n - 1) * (1 - f))
        def _():
            remote(flow.at[f], flow.at[f], flow_send.at[f], flow_recv.at[f, 0], right).wait_send()

    sec_sent = sec.at[pl.ds(0, lacking)]

    @pl.when(gone == 0)
    def _():
        for i in range(mids):
            affine_copy((1 - side) * mids + i, near_block).wait_send()
        remote(sec_sent, sec_sent, sec_send.at[0], sec_recv.at[0], right).wait_send()

    @pl.when(inner)
    def _():
        remote(sec_sent, sec_sent, sec_send.at[1], sec_recv.at[0], right).wait_send()

    stats_wait(nb, b, stat3, st3_send.at[0], st3_recv.at[0])
    mean3, var3 = combine(stat3[...], local)
    scale3 = gain3[...] / jnp.sqrt(var3 + eps)
    bias3_value = bias3[...]

    def finish(t, carry):
        kept = img[pl.ds(t * join, join)].reshape(tall, out_local).astype(f32)
        value = (third[t] - mean3) * scale3 + bias3_value + kept
        outv[t] = jnp.maximum(value, 0.0).astype(bf16)
        return carry

    lax.fori_loop(0, pieces, finish, 0)


def body(
    images,
    reduce_weight,
    reduce_gain,
    reduce_bias,
    spatial_weight,
    spatial_gain,
    spatial_bias,
    expand_weight,
    expand_gain,
    expand_bias,
):
    imgs, side = (images.shape[0], images.shape[1])
    n, nb = lax.axis_size("chan"), lax.axis_size("batch")
    width = reduce_weight.shape[1]
    depth = images.shape[3]
    out_local = expand_weight.shape[1]
    rows, height = side, side * imgs
    chunks = n * rows
    mid = n * width
    mids = n // 2
    more = EXTRA if mids > 1 else 0
    slots, lacking = mids + more, mids - more
    join = 2 if side % 2 == 0 else 1
    pieces, tall = side // join, height * join
    dma, f32, bf16 = pltpu.SemaphoreType.DMA, jnp.float32, jnp.bfloat16
    vmem = pl.BlockSpec(memory_space=pltpu.VMEM)
    anywhere = pl.BlockSpec(memory_space=pl.ANY)
    flat = images.transpose(1, 2, 0, 3).reshape(rows, height, depth)
    out = pl.pallas_call(
        functools.partial(block_kernel, n, nb, imgs),
        out_shape=pltpu.VMEM((pieces, tall, out_local), bf16),
        in_specs=[anywhere, anywhere, vmem, vmem, anywhere, vmem, vmem, anywhere, vmem, vmem],
        out_specs=vmem,
        scratch_shapes=[
            pltpu.VMEM((rows, height, depth), bf16),
            pltpu.VMEM(reduce_weight.shape, bf16),
            pltpu.VMEM((n, depth, width), bf16),
            pltpu.VMEM((chunks, height, width), f32),
            pltpu.VMEM((2, rows, height, width), f32),
            pltpu.VMEM((2, chunks, height, width), bf16),
            pltpu.VMEM((n, 4, width), f32),
        ]
        + [pltpu.VMEM((n, 1, width), f32)] * 3
        + [
            pltpu.VMEM((n, nb, 2, width), f32),
            pltpu.VMEM((n, rows + 2, height, width), bf16),
            pltpu.VMEM((slots, 3, 3, mid, width), bf16),
            pltpu.VMEM((slots, rows, height, width), f32),
            pltpu.VMEM((n, rows, height, width), bf16),
        ]
        + [pltpu.VMEM((slots, 1, width), f32)] * 3
        + [
            pltpu.VMEM((nb, lacking, 2, width), f32),
            pltpu.VMEM((nb, 2, 2, width), f32),
            pltpu.VMEM((n, 2, width), f32),
            pltpu.VMEM(expand_weight.shape, bf16),
            pltpu.VMEM((pieces, tall, out_local), f32),
        ]
        + [pltpu.VMEM((1, out_local), f32)] * 3
        + [pltpu.VMEM((nb, 2, out_local), f32)]
        + [dma((4,))]
        + [dma((1,))] * 2
        + [dma((1,)), dma((n,))]
        + [dma((n,))] * 4
        + [dma((2,)), dma((2, chunks))]
        + [dma((n,))] * 2
        + [dma((3,)), dma((slots, 3))]
        + [dma((slots,))] * 4
        + [dma((2,)), dma((lacking * rows,))]
        + [dma((1,))] * 4
        + [dma((n,)), dma((1,))]
        + [dma((1,))] * 2,
        compiler_params=pltpu.CompilerParams(
            collective_id=0, has_side_effects=True, vmem_limit_bytes=LIMIT
        ),
        name="block",
    )(
        flat,
        reduce_weight,
        reduce_gain[None, :],
        reduce_bias[None, :],
        spatial_weight,
        spatial_gain[None, :],
        spatial_bias[None, :],
        expand_weight,
        expand_gain[None, :],
        expand_bias[None, :],
    )
    return out.reshape(side, side, imgs, out_local).transpose(2, 0, 1, 3)


def solution(mesh):
    in_specs = (
        P("batch", None, None, "chan"),
        P(None, "chan"),
        P("chan"),
        P("chan"),
        P(None, None, None, "chan"),
        P("chan"),
        P("chan"),
        P(None, "chan"),
        P("chan"),
        P("chan"),
    )
    out_specs = P("batch", None, None, "chan")
    return jax.shard_map(body, mesh=mesh, in_specs=in_specs, out_specs=out_specs, check_vma=False)
```

time: 151 us -> 147 us (0.974)
  Pallas kernels: 149 us -> 145 us
    pallas_call x1, Pallas kernels: 149 us -> 145 us  [body(): pl.pallas_call(functools.partial(block_kernel, n, nb, imgs), out_shape=pl...]
where the time goes in v3:
time: 147 us
  Pallas kernels  145 us (99%)
  local copies, waits for them, and re-layouts  1.69 us (1%)
    pallas_call x1, Pallas kernels, body(): pl.pallas_call(functools.partial(block_kernel, n, nb, imgs), out_shape=pl...  145 us

profile of v3, /device:TPU:0, one launch (start us, length us, event | category | flops | bytes accessed | tf_op | source)
XLA Modules:
  0.0 146.6 jit_solution(1310114708703992231)
XLA Ops:
  0.0 144.9 %block.1 = bf16[7,224,1024]{2,1,0:T(8,128)(2,1)S(1)} custom-call(bf16[14,112,1024]{2,1,0:T(8,128)(2,1)} %bitcast.13, bf16[4096,256]{1,0:T(8,128)(2,1)} %w1_hbm.1, f32[1,256]{1,0:T(1,128)} %bitcast.16, f32[1,256]{1,0:T(1,128)} %bitcast.17, bf16[3,3,1024,256]{3,2,1,0:T(8,128)(2,1)} %sw_hbm.1, f32[1,256]{1,0:T(1,128)} %bitcast.18, f32[1,256]{1,0:T(1,128)} %bitcast.19, ...), custom_call_target="tpu_custom_call" | custom-call | tf_op jit(solution)/shard_map/block/pallas_call | solution.py:760
  144.9 1.7 %copy.12 = bf16[8,14,14,1024]{3,0,2,1:T(8,128)(2,1)} copy(bf16[8,14,14,1024]{3,0,2,1:T(8,128)(2,1)S(1)} %bitcast.12) | data formatting | bytes 6422528

commit v4 on v3

--- a/solution.py
+++ b/solution.py
@@ -14,11 +14,10 @@
 EXTRA = 1
 HELD = 4
 SETTLE = 8
-OUTER_GIVE = (0, 3, 6)
-INNER_SHARE = (0, 18, 22)
+INNER_SHARE = (0, 2, 4)
 OUTER_SHARE = (0, 2, 4)
-INNER_MORE = (1, 26, 33)
-OUTER_MORE = (21, 25, 33)
+INNER_MORE = (20, 26, 34)
+OUTER_MORE = (14, 23, 33)
 MORE_CHAIN = (1, 3, 5)
 
 
@@ -176,13 +175,7 @@
                 to = jnp.where(side == 0, mids, mids - 1)
                 w2_give(row_tap, to, jnp.where(side == 0, 0, mids), 1).start()
 
-        if row_tap == 0:
-            half_give(row_tap)
-        else:
-
-            @pl.when(inner)
-            def _():
-                half_give(row_tap)
+        half_give(row_tap)
 
     def strip_copy(g, who, send, recv, device):
         ref = wown.at[g, rows_of(who), :]
@@ -332,8 +325,7 @@
 
         return line
 
-    def convolve(g, t, slot):
-        lines = pl.ds(t * join, join)
+    def tap_products(g, t, slot):
         for col_tap in range(3):
             total = None
             for row_tap in range(3):
@@ -341,13 +333,22 @@
                 weight = w2[slot, row_tap, col_tap, pl.ds(pl.multiple_of(g * width, 128), width), :]
                 term = jnp.dot(window, weight, preferred_element_type=f32)
                 total = term if total is None else total + term
-            total = total.reshape(join, height, width)
-            if col_tap == 0:
-                acc[slot, lines, imgs:, :] += total[:, : height - imgs]
-            elif col_tap == 1:
-                acc[slot, lines] += total
-            else:
-                acc[slot, lines, : height - imgs, :] += total[:, imgs:]
+            yield total.reshape(join, height, width)
+
+    def convolve(g, t, slot):
+        lines = pl.ds(t * join, join)
+        left, middle, right = tap_products(g, t, slot)
+        acc[slot, lines, imgs:, :] += left[:, : height - imgs]
+        acc[slot, lines] += middle
+        acc[slot, lines, : height - imgs, :] += right[:, imgs:]
+
+    def convolve_last(t, slot):
+        left, middle, right = tap_products(last, t, slot)
+        edge = jnp.zeros((join, imgs, width), f32)
+        total = acc[slot, pl.ds(t * join, join)] + middle
+        total = total + jnp.concatenate([edge, left[:, : height - imgs]], axis=1)
+        total = total + jnp.concatenate([right[:, imgs:], edge], axis=1)
+        return total.reshape(tall, width)
 
     last = n - 1
     all_begin = last * rows - pieces + 1
@@ -362,12 +363,6 @@
                 forward(g)
 
         for row_tap in range(3):
-            if row_tap:
-
-                @pl.when(jnp.logical_and(at_end, s == OUTER_GIVE[row_tap]))
-                def _():
-                    half_give(row_tap)
-
             if more:
 
                 @pl.when(s == jnp.where(at_end, OUTER_MORE[row_tap], MORE_CHAIN[row_tap]))
@@ -431,7 +426,7 @@
             def _():
                 finalize(late, part[late] + coming)
 
-        @pl.when(after == half_begin - 6)
+        @pl.when(after == half_begin - 4)
         def _():
             half_slots(w2_forward)
 
@@ -526,22 +521,20 @@
                 sec_copy(1 - side, u).start()
 
     line = first_affine(last)
-    line(0)
-    sum2[...] = jnp.zeros_like(sum2)
-    square2[...] = jnp.zeros_like(square2)
-
-    def measure(t, slot):
-        convolve(last, t, slot)
+
+    def measure(t, slot, fresh):
+        total = convolve_last(t, slot)
+        if fresh:
+            shift2[slot] = column_sum(total) / tall
+        moved = total - shift2[slot]
+        sums, squares = column_sum(moved), column_sum(moved * moved)
+        if fresh:
+            sum2[slot] = sums
+            square2[slot] = squares
+        else:
+            sum2[slot] += sums
+            square2[slot] += squares
         lines = pl.ds(t * join, join)
-        total = acc[slot, lines].reshape(tall, width)
-
-        @pl.when(t == 0)
-        def _():
-            shift2[slot] = column_sum(total) / tall
-
-        moved = total - shift2[slot]
-        sum2[slot] += column_sum(moved)
-        square2[slot] += column_sum(moved * moved)
         sec[first_block + slot, lines] = moved.astype(bf16).reshape(join, height, width)
 
     def record(stats, i, slot):
@@ -558,37 +551,40 @@
             affine[block, 0:1, :] = scale
             affine[block, 1:2, :] = (shift2[base + i] - mean[i]) * scale + gb[block, 3:4, :]
 
-    def outgoing(t, carry):
+    def outgoing(t, fresh):
         for ahead in range(1, join + 1):
-
-            @pl.when(t * join + ahead < rows)
-            def _():
-                line(t * join + ahead)
-
+            line(jnp.minimum(t * join + ahead, rows - 1))
         for i in range(lacking):
-            measure(t, out_slot + i)
+            measure(t, out_slot + i, fresh)
 
         @pl.when(jnp.logical_and(gone == 0, t < HELD))
         def _():
             lax.fori_loop(t * per_piece, (t + 1) * per_piece, sec_start, 0)
 
+    def outgoing_next(t, carry):
+        outgoing(t, False)
         return carry
 
-    lax.fori_loop(0, pieces, outgoing, 0)
+    line(0)
+    outgoing(0, True)
+    lax.fori_loop(1, pieces, outgoing_next, 0)
     for i in range(lacking):
         record(stat_out, i, out_slot + i)
     stats_send(nb, b, stat_out, st2_send.at[0], st2_recv.at[0])
 
-    def keeping(t, carry):
+    def keeping(t, fresh):
+        relay(t)
         for i in range(2 * more):
-            measure(t, keep_slot + i)
-
-        relay(t)
+            measure(t, keep_slot + i, fresh)
+
+    def keeping_next(t, carry):
+        keeping(t, False)
         return carry
 
-    begun = pieces // 2 if more else 0
+    begun = max(pieces // 2, 1)
     if more:
-        lax.fori_loop(0, begun, keeping, 0)
+        keeping(0, True)
+        lax.fori_loop(1, begun, keeping_next, 0)
     stats_wait(nb, b, stat_out, st2_send.at[0], st2_recv.at[0])
     derive(stat_out, out_slot, lacking)
 
@@ -599,7 +595,7 @@
         lax.fori_loop(min(HELD, pieces) * per_piece, units, sec_start, 0)
 
     if more:
-        lax.fori_loop(begun, pieces, keeping, 0)
+        lax.fori_loop(begun, pieces, keeping_next, 0)
         for i in range(2 * more):
             record(stat_keep, i, keep_slot + i)
         stats_send(nb, b, stat_keep, st4_send.at[0], st4_recv.at[0])

time: 147 us -> 139 us (0.946)
  Pallas kernels: 145 us -> 137 us
    pallas_call x1, Pallas kernels: 145 us -> 137 us  [body(): pl.pallas_call(functools.partial(block_kernel, n, nb, imgs), out_shape=pl...]
where the time goes in v4:
time: 139 us
  Pallas kernels  137 us (99%)
  local copies, waits for them, and re-layouts  1.69 us (1%)
    pallas_call x1, Pallas kernels, body(): pl.pallas_call(functools.partial(block_kernel, n, nb, imgs), out_shape=pl...  137 us

profile of v4, /device:TPU:0, one launch (start us, length us, event | category | flops | bytes accessed | tf_op | source)
XLA Modules:
  0.0 138.7 jit_solution(18226804656635051967)
XLA Ops:
  0.0 137.0 %block.1 = bf16[7,224,1024]{2,1,0:T(8,128)(2,1)S(1)} custom-call(bf16[14,112,1024]{2,1,0:T(8,128)(2,1)} %bitcast.13, bf16[4096,256]{1,0:T(8,128)(2,1)} %w1_hbm.1, f32[1,256]{1,0:T(1,128)} %bitcast.16, f32[1,256]{1,0:T(1,128)} %bitcast.17, bf16[3,3,1024,256]{3,2,1,0:T(8,128)(2,1)} %sw_hbm.1, f32[1,256]{1,0:T(1,128)} %bitcast.18, f32[1,256]{1,0:T(1,128)} %bitcast.19, ...), custom_call_target="tpu_custom_call" | custom-call | tf_op jit(solution)/shard_map/block/pallas_call | solution.py:756
  137.1 1.7 %copy.12 = bf16[8,14,14,1024]{3,0,2,1:T(8,128)(2,1)} copy(bf16[8,14,14,1024]{3,0,2,1:T(8,128)(2,1)S(1)} %bitcast.12) | data formatting | bytes 6422528

commit v5 on v4

--- a/solution.py
+++ b/solution.py
@@ -13,11 +13,13 @@
 SKEW = 3
 EXTRA = 1
 HELD = 4
-SETTLE = 8
-INNER_SHARE = (0, 2, 4)
+SETTLE = 5
+AHEAD = 4
+PARTIAL = 4
+INNER_SHARE = (0, 2, 9)
 OUTER_SHARE = (0, 2, 4)
 INNER_MORE = (20, 26, 34)
-OUTER_MORE = (14, 23, 33)
+OUTER_MORE = (14, 23, 37)
 MORE_CHAIN = (1, 3, 5)
 
 
@@ -67,11 +69,12 @@
 
 def block_kernel(
     n, nb, imgs,
-    img_hbm, w1_hbm, gain1, bias1, sw_hbm, gain2, bias2, w3_hbm, gain3, bias3,
+    img_hbm, w1_hbm, gain1_hbm, bias1_hbm, sw_hbm, gain2_hbm, bias2_hbm, w3_hbm, gain3_hbm, bias3_hbm,
     outv,
     img, w1, wown, part, whole, flow, gb, shift1, sum1, square1, stat1, act, w2, acc, sec,
     shift2, sum2, square2, stat_out, stat_keep, affine, w3, third, shift3, sum3, square3, stat3,
-    load_sem,
+    gain1, bias1, gain2, bias2, gain3, bias3,
+    load_sem, small_sem,
     gb_send, gb_recv, w1_send, w1_recv, hop_send, hop_recv, pair_send, pair_recv,
     flow_send, flow_recv, st1_send, st1_recv,
     w2_send, w2_recv, w2hop_send, w2hop_recv, w2pair_send, w2pair_recv,
@@ -119,11 +122,22 @@
 
     w2_load = pltpu.make_async_copy(sw_hbm, w2.at[my_slot], load_sem.at[3])
     w2_load.start()
+    pairs = [
+        (gain1_hbm, gain1), (bias1_hbm, bias1), (gain2_hbm, gain2),
+        (bias2_hbm, bias2), (gain3_hbm, gain3), (bias3_hbm, bias3),
+    ]
+    small = [
+        pltpu.make_async_copy(src, dst, small_sem.at[i]) for i, (src, dst) in enumerate(pairs)
+    ]
+    for copy in small:
+        copy.start()
+    greet(n, nb, z, b)
+    for copy in small:
+        copy.wait()
     gb[z, 0:1, :] = gain1[...]
     gb[z, 1:2, :] = bias1[...]
     gb[z, 2:3, :] = gain2[...]
     gb[z, 3:4, :] = bias2[...]
-    greet(n, nb, z, b)
 
     def rows_of(who):
         return pl.ds(pl.multiple_of(who * strip, 16), strip)
@@ -175,7 +189,13 @@
                 to = jnp.where(side == 0, mids, mids - 1)
                 w2_give(row_tap, to, jnp.where(side == 0, 0, mids), 1).start()
 
-        half_give(row_tap)
+        if row_tap < 2:
+            half_give(row_tap)
+        else:
+
+            @pl.when(inner)
+            def _():
+                half_give(row_tap)
 
     def strip_copy(g, who, send, recv, device):
         ref = wown.at[g, rows_of(who), :]
@@ -232,7 +252,13 @@
 
         return carry
 
-    lax.fori_loop(0, rows, own_products, 0)
+    lax.fori_loop(0, min(AHEAD, rows), own_products, 0)
+
+    @pl.when(at_first)
+    def _():
+        half_give(2)
+
+    lax.fori_loop(min(AHEAD, rows), rows, own_products, 0)
     for g in range(n):
         distribute(g)
     act[:, 0] = jnp.zeros_like(act[:, 0])
@@ -351,11 +377,15 @@
         return total.reshape(tall, width)
 
     last = n - 1
-    all_begin = last * rows - pieces + 1
-    more_begin = all_begin - pieces
-    half_begin = more_begin - (last - 1) * pieces
-
-    def step(s, carry):
+    all_begin = (last - 1) * rows + SETTLE + 1
+    more_begin = all_begin - pieces + 1
+    half_begin = SETTLE + 2
+
+    def prepare(s):
+        @pl.when(jnp.logical_and(at_last, s == AHEAD // 2))
+        def _():
+            half_give(2)
+
         for g in range(1, n):
 
             @pl.when(s == (g - 1) * (rows // 2) + 2)
@@ -400,6 +430,7 @@
                     flow[side, k] = part[k].astype(bf16)
                     flow_copy(side, k).start()
 
+    def step(s, carry):
         early = s - early_skew
 
         @pl.when(jnp.logical_and(inner, jnp.logical_and(early >= 0, early < chunks)))
@@ -469,10 +500,12 @@
 
         item = after - half_begin
 
-        @pl.when(jnp.logical_and(item >= 0, item < (last - 1) * pieces))
+        turn = lax.rem(item, rows)
+
+        @pl.when(jnp.logical_and(item >= 0, jnp.logical_and(item < (last - 1) * rows, turn < pieces)))
         def _():
             for i in range(mids):
-                convolve(lax.div(item, pieces), lax.rem(item, pieces), half_slot + i)
+                convolve(lax.div(item, rows), turn, half_slot + i)
 
         if more:
 
@@ -481,14 +514,25 @@
                 for g in range(last - 1):
                     convolve(g, after - more_begin, more_slot)
 
-        @pl.when(after >= all_begin)
+        since = after - all_begin
+        t = lax.div(3 * since + 3, 4)
+
+        @pl.when(jnp.logical_and(since >= 0, jnp.logical_and(t < pieces, lax.div(4 * t, 3) == since)))
         def _():
             for slot in range(slots):
-                convolve(last - 1, after - all_begin, slot)
+                convolve(last - 1, t, slot)
 
         return carry
 
-    lax.fori_loop(0, chunks + late_skew, step, 0)
+    def first_step(s, carry):
+        prepare(s)
+        return step(s, carry)
+
+    settled = max(
+        chunks // 2, max(OUTER_MORE) + 1, max(INNER_MORE) + 1, (n - 2) * (rows // 2) + 3
+    )
+    lax.fori_loop(0, settled, first_step, 0)
+    lax.fori_loop(settled, chunks + late_skew, step, 0)
 
     def sec_copy(f, u):
         to = jnp.where(f == 0, lax.rem(z + 1, n), lax.rem(z + n - 1, n))
@@ -594,69 +638,112 @@
             affine_copy((1 - side) * mids + i, near_block).start()
         lax.fori_loop(min(HELD, pieces) * per_piece, units, sec_start, 0)
 
+    part_count = PARTIAL
+    if not more or per_piece * PARTIAL > pieces + PARTIAL - SKEW * (mids - 1):
+        part_count = 0
+    w3_load.wait()
+    sum3[...] = jnp.zeros_like(sum3)
+    square3[...] = jnp.zeros_like(square3)
+    outer_blocks = list(range(lacking)) + list(range(mids + more, n))
+    inner_blocks = list(range(lacking, mids + more))
+
+    def product(t, blocks):
+        total = None
+        while blocks:
+            run = [blocks[0]]
+            while run[-1] + 1 in blocks:
+                run.append(run[-1] + 1)
+            blocks = [block for block in blocks if block not in run]
+            values = []
+            for block in run:
+                value = sec[block, pl.ds(t * join, join)].reshape(tall, width).astype(f32)
+                value = value * affine[block, 0:1, :] + affine[block, 1:2, :]
+                values.append(jnp.maximum(value, 0.0).astype(bf16))
+            lines = slice(run[0] * width, (run[-1] + 1) * width)
+            term = jnp.dot(
+                jnp.concatenate(values, axis=1), w3[lines, :], preferred_element_type=f32
+            )
+            total = term if total is None else total + term
+        return total
+
+    def settle(t, total, fresh):
+        if fresh:
+            shift3[...] = column_sum(total) / tall
+        moved = total - shift3[...]
+        third[t] = moved
+        sum3[...] += column_sum(moved)
+        square3[...] += column_sum(moved * moved)
+
+    def far_affine():
+        ref = affine.at[pl.ds(far_block, lacking)]
+        return remote(ref, ref, aff_send.at[0], aff_recv.at[0], {"chan": lax.rem(z + 1, n)})
+
     if more:
         lax.fori_loop(begun, pieces, keeping_next, 0)
         for i in range(2 * more):
             record(stat_keep, i, keep_slot + i)
         stats_send(nb, b, stat_keep, st4_send.at[0], st4_recv.at[0])
-        for tick in range(pieces, pieces + 2):
-            relay(tick)
+        if part_count:
+            far_affine().wait_recv()
+
+            def part_step(t, carry):
+                relay(pieces + t)
+                third[t] = product(t, outer_blocks)
+                return carry
+
+            lax.fori_loop(0, part_count, part_step, 0)
+        else:
+            for tick in range(pieces, pieces + 2):
+                relay(tick)
         stats_wait(nb, b, stat_keep, st4_send.at[0], st4_recv.at[0])
         derive(stat_keep, keep_slot, 2 * more)
 
-    w3_load.wait()
-    sum3[...] = jnp.zeros_like(sum3)
-    square3[...] = jnp.zeros_like(square3)
     lag = SKEW * gone
-
-    def expand(t):
-        values = []
-        for block in range(n):
-            value = sec[block, pl.ds(t * join, join)].reshape(tall, width).astype(f32)
-            value = value * affine[block, 0:1, :] + affine[block, 1:2, :]
-            values.append(jnp.maximum(value, 0.0).astype(bf16))
-        total = jnp.dot(
-            jnp.concatenate(values, axis=1), w3[...], preferred_element_type=f32
-        )
-        third[t] = total
-
-        @pl.when(t == 0)
-        def _():
-            shift3[...] = column_sum(total) / tall
-
-        moved = third[t] - shift3[...]
-        sum3[...] += column_sum(moved)
-        square3[...] += column_sum(moved * moved)
-
-    relay_first = pieces + 2 if more else 0
-    ready = relay_first + 1
+    relay_first = pieces + (part_count or 2) if more else 0
+    if part_count:
+        settle(0, third[0] + product(0, inner_blocks), True)
+
+        def rest_step(t, carry):
+            settle(t, third[t] + product(t, inner_blocks), False)
+            return carry
+
+        lax.fori_loop(1, part_count, rest_step, 0)
+    ready = relay_first if part_count else relay_first + 1
 
     def relay_step(s, carry):
         relay(s)
-
-        @pl.when(s == ready)
-        def _():
-            remote(
-                affine.at[pl.ds(far_block, lacking)], affine.at[pl.ds(far_block, lacking)],
-                aff_send.at[0], aff_recv.at[0], {"chan": lax.rem(z + 1, n)},
-            ).wait_recv()
-
-        t_late = s - ready
-        catching = jnp.logical_and(t_late >= 0, t_late < pieces)
+        if not part_count:
+
+            @pl.when(s == ready)
+            def _():
+                far_affine().wait_recv()
+
+        t_late = s - ready + part_count
+        catching = jnp.logical_and(s >= ready, t_late < pieces)
         catching = jnp.logical_and(catching, per_piece * (t_late + 1) - 1 + lag <= s)
         fresh = s - (per_piece - 1) - lag
         t_fresh = lax.div(fresh, per_piece)
         arriving = jnp.logical_and(fresh >= 0, lax.rem(fresh, per_piece) == 0)
         arriving = jnp.logical_and(arriving, t_fresh < pieces)
-        arriving = jnp.logical_and(arriving, ready + t_fresh < s)
-
-        @pl.when(jnp.logical_or(catching, arriving))
-        def _():
-            expand(jnp.where(catching, t_late, t_fresh))
+        arriving = jnp.logical_and(arriving, ready + t_fresh - part_count < s)
+        arriving = jnp.logical_and(arriving, t_fresh >= part_count)
+        t = jnp.where(catching, t_late, t_fresh)
+        due = jnp.logical_or(catching, arriving)
+        if not part_count:
+
+            @pl.when(jnp.logical_and(due, t == 0))
+            def _():
+                settle(t, product(t, list(range(n))), True)
+
+            due = jnp.logical_and(due, t > 0)
+
+        @pl.when(due)
+        def _():
+            settle(t, product(t, list(range(n))), False)
 
         return carry
 
-    relay_last = jnp.maximum(units + lag, ready + pieces)
+    relay_last = jnp.maximum(units + lag, ready + pieces - part_count)
     lax.fori_loop(relay_first, relay_last, relay_step, 0)
 
     extra = sum3[...] / local
@@ -713,11 +800,11 @@
     stats_wait(nb, b, stat3, st3_send.at[0], st3_recv.at[0])
     mean3, var3 = combine(stat3[...], local)
     scale3 = gain3[...] / jnp.sqrt(var3 + eps)
-    bias3_value = bias3[...]
+    offset3 = (shift3[...] - mean3) * scale3 + bias3[...]
 
     def finish(t, carry):
         kept = img[pl.ds(t * join, join)].reshape(tall, out_local).astype(f32)
-        value = (third[t] - mean3) * scale3 + bias3_value + kept
+        value = third[t] * scale3 + offset3 + kept
         outv[t] = jnp.maximum(value, 0.0).astype(bf16)
         return carry
 
@@ -756,7 +843,7 @@
     out = pl.pallas_call(
         functools.partial(block_kernel, n, nb, imgs),
         out_shape=pltpu.VMEM((pieces, tall, out_local), bf16),
-        in_specs=[anywhere, anywhere, vmem, vmem, anywhere, vmem, vmem, anywhere, vmem, vmem],
+        in_specs=[anywhere] * 10,
         out_specs=vmem,
         scratch_shapes=[
             pltpu.VMEM((rows, height, depth), bf16),
@@ -785,7 +872,9 @@
         ]
         + [pltpu.VMEM((1, out_local), f32)] * 3
         + [pltpu.VMEM((nb, 2, out_local), f32)]
-        + [dma((4,))]
+        + [pltpu.VMEM((1, width), f32)] * 4
+        + [pltpu.VMEM((1, out_local), f32)] * 2
+        + [dma((4,)), dma((6,))]
         + [dma((1,))] * 2
         + [dma((1,)), dma((n,))]
         + [dma((n,))] * 4

time: 139 us -> 135 us (0.971)
  Pallas kernels: 137 us -> 133 us
    pallas_call x1, Pallas kernels: 137 us -> 133 us  [body(): pl.pallas_call(functools.partial(block_kernel, n, nb, imgs), out_shape=pl...]
where the time goes in v5:
time: 135 us
  Pallas kernels  133 us (99%)
  local copies, waits for them, and re-layouts  1.69 us (1%)
    pallas_call x1, Pallas kernels, body(): pl.pallas_call(functools.partial(block_kernel, n, nb, imgs), out_shape=pl...  133 us

profile of v5, /device:TPU:0, one launch (start us, length us, event | category | flops | bytes accessed | tf_op | source)
XLA Modules:
  0.0 135.1 jit_solution(14697476896421433800)
XLA Ops:
  0.0 133.4 %block.1 = bf16[7,224,1024]{2,1,0:T(8,128)(2,1)S(1)} custom-call(bf16[14,112,1024]{2,1,0:T(8,128)(2,1)} %bitcast.13, bf16[4096,256]{1,0:T(8,128)(2,1)} %w1_hbm.1, f32[1,256]{1,0:T(1,128)} %bitcast.16, f32[1,256]{1,0:T(1,128)} %bitcast.17, bf16[3,3,1024,256]{3,2,1,0:T(8,128)(2,1)} %sw_hbm.1, f32[1,256]{1,0:T(1,128)} %bitcast.18, f32[1,256]{1,0:T(1,128)} %bitcast.19, ...), custom_call_target="tpu_custom_call" | custom-call | tf_op jit(solution)/shard_map/block/pallas_call | solution.py:843
  133.4 1.7 %copy.12 = bf16[8,14,14,1024]{3,0,2,1:T(8,128)(2,1)} copy(bf16[8,14,14,1024]{3,0,2,1:T(8,128)(2,1)S(1)} %bitcast.12) | data formatting | bytes 6422528

commit v6 on v5

--- a/solution.py
+++ b/solution.py
@@ -14,9 +14,9 @@
 EXTRA = 1
 HELD = 4
 SETTLE = 5
-AHEAD = 4
+AHEAD = 8
 PARTIAL = 4
-INNER_SHARE = (0, 2, 9)
+INNER_SHARE = (0, 2, 11)
 OUTER_SHARE = (0, 2, 4)
 INNER_MORE = (20, 26, 34)
 OUTER_MORE = (14, 23, 37)
@@ -73,8 +73,8 @@
     outv,
     img, w1, wown, part, whole, flow, gb, shift1, sum1, square1, stat1, act, w2, acc, sec,
     shift2, sum2, square2, stat_out, stat_keep, affine, w3, third, shift3, sum3, square3, stat3,
-    gain1, bias1, gain2, bias2, gain3, bias3,
-    load_sem, small_sem,
+    gain1, bias1, gain2, bias2, gain3, bias3, norm,
+    load_sem, small_sem, norm_send, norm_recv,
     gb_send, gb_recv, w1_send, w1_recv, hop_send, hop_recv, pair_send, pair_recv,
     flow_send, flow_recv, st1_send, st1_recv,
     w2_send, w2_recv, w2hop_send, w2hop_recv, w2pair_send, w2pair_recv,
@@ -339,11 +339,14 @@
         stat1[g, b, 1:2, :] = square1[g] - sum1[g] * extra
         stats_send(nb, b, stat1.at[g], st1_send.at[g], st1_recv.at[g])
 
-    def first_affine(g):
+    def first_scale(g, kept):
         stats_wait(nb, b, stat1.at[g], st1_send.at[g], st1_recv.at[g])
         mean, var = combine(stat1[g], local)
-        scale = gb[g, 0:1, :] / jnp.sqrt(var + eps)
-        bias = gb[g, 1:2, :]
+        norm[kept, 0:1, :] = mean
+        norm[kept, 1:2, :] = gb[g, 0:1, :] / jnp.sqrt(var + eps)
+
+    def first_affine(g, kept):
+        mean, scale, bias = norm[kept, 0:1, :], norm[kept, 1:2, :], gb[g, 1:2, :]
 
         def line(r):
             value = (whole[lax.rem(g, 2), r] - mean) * scale + bias
@@ -377,8 +380,9 @@
         return total.reshape(tall, width)
 
     last = n - 1
-    all_begin = (last - 1) * rows + SETTLE + 1
-    more_begin = all_begin - pieces + 1
+    own_last = inner if mids > 1 else z >= 0
+    all_begin = last * rows - pieces + 1
+    more_begin = all_begin - pieces
     half_begin = SETTLE + 2
 
     def prepare(s):
@@ -480,7 +484,7 @@
         def _():
             g, v = lax.div(after, rows), lax.rem(after, rows)
 
-            @pl.when(v == 0)
+            @pl.when(jnp.logical_and(v == 0, jnp.logical_or(own_last, g < last)))
             def _():
                 first_stats(g)
 
@@ -490,7 +494,8 @@
                 def _():
                     gb_all().wait_recv()
 
-                line = first_affine(g)
+                first_scale(g, 0)
+                line = first_affine(g, 0)
 
                 def each_line(r, carry):
                     line(r)
@@ -514,13 +519,10 @@
                 for g in range(last - 1):
                     convolve(g, after - more_begin, more_slot)
 
-        since = after - all_begin
-        t = lax.div(3 * since + 3, 4)
-
-        @pl.when(jnp.logical_and(since >= 0, jnp.logical_and(t < pieces, lax.div(4 * t, 3) == since)))
+        @pl.when(after >= all_begin)
         def _():
             for slot in range(slots):
-                convolve(last - 1, t, slot)
+                convolve(last - 1, after - all_begin, slot)
 
         return carry
 
@@ -564,7 +566,25 @@
             def _():
                 sec_copy(1 - side, u).start()
 
-    line = first_affine(last)
+    to_end = jnp.where(side == 0, 0, n - 1)
+    next_to_end = jnp.logical_and(inner, jnp.logical_or(z == 1, z == n - 2))
+    norm_copy = remote(norm.at[1], norm.at[1], norm_send.at[0], norm_recv.at[0], {"chan": to_end})
+
+    @pl.when(own_last)
+    def _():
+        first_scale(last, 1)
+
+    if mids > 1:
+
+        @pl.when(next_to_end)
+        def _():
+            norm_copy.start()
+
+        @pl.when(at_end)
+        def _():
+            norm_copy.wait_recv()
+
+    line = first_affine(last, 1)
 
     def measure(t, slot, fresh):
         total = convolve_last(t, slot)
@@ -629,11 +649,13 @@
     if more:
         keeping(0, True)
         lax.fori_loop(1, begun, keeping_next, 0)
-    stats_wait(nb, b, stat_out, st2_send.at[0], st2_recv.at[0])
-    derive(stat_out, out_slot, lacking)
+    def take_out_stats():
+        stats_wait(nb, b, stat_out, st2_send.at[0], st2_recv.at[0])
+        derive(stat_out, out_slot, lacking)
 
     @pl.when(gone == 0)
     def _():
+        take_out_stats()
         for i in range(mids):
             affine_copy((1 - side) * mids + i, near_block).start()
         lax.fori_loop(min(HELD, pieces) * per_piece, units, sec_start, 0)
@@ -680,6 +702,11 @@
 
     if more:
         lax.fori_loop(begun, pieces, keeping_next, 0)
+    @pl.when(gone > 0)
+    def _():
+        take_out_stats()
+
+    if more:
         for i in range(2 * more):
             record(stat_keep, i, keep_slot + i)
         stats_send(nb, b, stat_keep, st4_send.at[0], st4_recv.at[0])
@@ -701,14 +728,25 @@
     lag = SKEW * gone
     relay_first = pieces + (part_count or 2) if more else 0
     if part_count:
+
+        def rest_relay(t):
+            @pl.when(gone == 0)
+            def _():
+                relay(relay_first + t)
+
+        rest_relay(0)
         settle(0, third[0] + product(0, inner_blocks), True)
 
         def rest_step(t, carry):
+            rest_relay(t)
             settle(t, third[t] + product(t, inner_blocks), False)
             return carry
 
         lax.fori_loop(1, part_count, rest_step, 0)
-    ready = relay_first if part_count else relay_first + 1
+    if part_count:
+        ready = relay_from = jnp.where(gone == 0, relay_first + part_count, relay_first)
+    else:
+        ready, relay_from = relay_first + 1, relay_first
 
     def relay_step(s, carry):
         relay(s)
@@ -744,7 +782,7 @@
         return carry
 
     relay_last = jnp.maximum(units + lag, ready + pieces - part_count)
-    lax.fori_loop(relay_first, relay_last, relay_step, 0)
+    lax.fori_loop(relay_from, relay_last, relay_step, 0)
 
     extra = sum3[...] / local
     stat3[b, 0:1, :] = shift3[...] + extra
@@ -784,6 +822,12 @@
         @pl.when(z != (n - 1) * (1 - f))
         def _():
             remote(flow.at[f], flow.at[f], flow_send.at[f], flow_recv.at[f, 0], right).wait_send()
+
+    if mids > 1:
+
+        @pl.when(next_to_end)
+        def _():
+            norm_copy.wait_send()
 
     sec_sent = sec.at[pl.ds(0, lacking)]
 
@@ -874,7 +918,8 @@
         + [pltpu.VMEM((nb, 2, out_local), f32)]
         + [pltpu.VMEM((1, width), f32)] * 4
         + [pltpu.VMEM((1, out_local), f32)] * 2
-        + [dma((4,)), dma((6,))]
+        + [pltpu.VMEM((2, 2, width), f32)]
+        + [dma((4,)), dma((6,)), dma((1,)), dma((1,))]
         + [dma((1,))] * 2
         + [dma((1,)), dma((n,))]
         + [dma((n,))] * 4

time: 135 us -> 134 us (level)
  no operation moved by 1% of the time
where the time goes in v6:
time: 134 us
  Pallas kernels  132 us (99%)
  local copies, waits for them, and re-layouts  1.69 us (1%)
    pallas_call x1, Pallas kernels, body(): pl.pallas_call(functools.partial(block_kernel, n, nb, imgs), out_shape=pl...  132 us

profile of v6, /device:TPU:0, one launch (start us, length us, event | category | flops | bytes accessed | tf_op | source)
XLA Modules:
  0.0 134.1 jit_solution(136033804777956271)
XLA Ops:
  0.0 132.4 %block.1 = bf16[7,224,1024]{2,1,0:T(8,128)(2,1)S(1)} custom-call(bf16[14,112,1024]{2,1,0:T(8,128)(2,1)} %bitcast.13, bf16[4096,256]{1,0:T(8,128)(2,1)} %w1_hbm.1, f32[1,256]{1,0:T(1,128)} %bitcast.16, f32[1,256]{1,0:T(1,128)} %bitcast.17, bf16[3,3,1024,256]{3,2,1,0:T(8,128)(2,1)} %sw_hbm.1, f32[1,256]{1,0:T(1,128)} %bitcast.18, f32[1,256]{1,0:T(1,128)} %bitcast.19, ...), custom_call_target="tpu_custom_call" | custom-call | tf_op jit(solution)/shard_map/block/pallas_call | solution.py:887
  132.5 1.7 %copy.12 = bf16[8,14,14,1024]{3,0,2,1:T(8,128)(2,1)} copy(bf16[8,14,14,1024]{3,0,2,1:T(8,128)(2,1)S(1)} %bitcast.12) | data formatting | bytes 6422528

commit v7 on v6

--- a/solution.py
+++ b/solution.py
@@ -536,16 +536,20 @@
     lax.fori_loop(0, settled, first_step, 0)
     lax.fori_loop(settled, chunks + late_skew, step, 0)
 
-    def sec_copy(f, u):
+    halves = 2 if width % 256 == 0 else 1
+    thin = width // halves
+
+    def sec_copy(f, u, part_of):
         to = jnp.where(f == 0, lax.rem(z + 1, n), lax.rem(z + n - 1, n))
         t, rest = lax.div(u, per_piece), lax.rem(u, per_piece)
         block = lax.div(rest, join) + f * (mids + more)
-        ref = sec.at[block, t * join + lax.rem(rest, join)]
+        ref = sec.at[block, t * join + lax.rem(rest, join), :, pl.ds(part_of * thin, thin)]
         kind = jnp.where(f == side, 0, 1)
-        return remote(ref, ref, sec_send.at[kind], sec_recv.at[u], {"chan": to})
+        return remote(ref, ref, sec_send.at[kind], sec_recv.at[u, part_of], {"chan": to})
 
     def sec_start(u, carry):
-        sec_copy(side, u).start()
+        for part_of in range(halves):
+            sec_copy(side, u, part_of).start()
         return carry
 
     far_block = (1 - side) * (mids + more)
@@ -560,11 +564,10 @@
 
         @pl.when(jnp.logical_and(u >= 0, u < units))
         def _():
-            sec_copy(1 - side, u).wait_recv()
-
-            @pl.when(inner)
-            def _():
-                sec_copy(1 - side, u).start()
+            for part_of in range(halves):
+                coming = sec_copy(1 - side, u, part_of)
+                coming.wait_recv()
+                pl.when(inner)(coming.start)
 
     to_end = jnp.where(side == 0, 0, n - 1)
     next_to_end = jnp.logical_and(inner, jnp.logical_or(z == 1, z == n - 2))
@@ -835,11 +838,11 @@
     def _():
         for i in range(mids):
             affine_copy((1 - side) * mids + i, near_block).wait_send()
-        remote(sec_sent, sec_sent, sec_send.at[0], sec_recv.at[0], right).wait_send()
+        remote(sec_sent, sec_sent, sec_send.at[0], sec_recv.at[0, 0], right).wait_send()
 
     @pl.when(inner)
     def _():
-        remote(sec_sent, sec_sent, sec_send.at[1], sec_recv.at[0], right).wait_send()
+        remote(sec_sent, sec_sent, sec_send.at[1], sec_recv.at[0, 0], right).wait_send()
 
     stats_wait(nb, b, stat3, st3_send.at[0], st3_recv.at[0])
     mean3, var3 = combine(stat3[...], local)
@@ -927,7 +930,7 @@
         + [dma((n,))] * 2
         + [dma((3,)), dma((slots, 3))]
         + [dma((slots,))] * 4
-        + [dma((2,)), dma((lacking * rows,))]
+        + [dma((2,)), dma((lacking * rows, 2))]
         + [dma((1,))] * 4
         + [dma((n,)), dma((1,))]
         + [dma((1,))] * 2,

time: 134 us -> 134 us (level)
  no operation moved by 1% of the time
where the time goes in v7:
time: 134 us
  Pallas kernels  133 us (99%)
  local copies, waits for them, and re-layouts  1.69 us (1%)
    pallas_call x1, Pallas kernels, body(): pl.pallas_call(functools.partial(block_kernel, n, nb, imgs), out_shape=pl...  133 us

profile of v7, /device:TPU:0, one launch (start us, length us, event | category | flops | bytes accessed | tf_op | source)
XLA Modules:
  0.0 134.2 jit_solution(3134886849613480224)
XLA Ops:
  0.0 132.5 %block.1 = bf16[7,224,1024]{2,1,0:T(8,128)(2,1)S(1)} custom-call(bf16[14,112,1024]{2,1,0:T(8,128)(2,1)} %bitcast.13, bf16[4096,256]{1,0:T(8,128)(2,1)} %w1_hbm.1, f32[1,256]{1,0:T(1,128)} %bitcast.16, f32[1,256]{1,0:T(1,128)} %bitcast.17, bf16[3,3,1024,256]{3,2,1,0:T(8,128)(2,1)} %sw_hbm.1, f32[1,256]{1,0:T(1,128)} %bitcast.18, f32[1,256]{1,0:T(1,128)} %bitcast.19, ...), custom_call_target="tpu_custom_call" | custom-call | tf_op jit(solution)/shard_map/block/pallas_call | solution.py:890
  132.5 1.7 %copy.12 = bf16[8,14,14,1024]{3,0,2,1:T(8,128)(2,1)} copy(bf16[8,14,14,1024]{3,0,2,1:T(8,128)(2,1)S(1)} %bitcast.12) | data formatting | bytes 6422528
